TPU v7x, 512 devices: a whole 4x8x8 slice. The times are simulated.
512 devices in a mesh: blk: 128 (over z_hi, x, y), chan: 4 (over z_lo, core).
Axes of the slice: x: 4, y: 8, z: 8 (z_hi: 4, z_lo: 2; z = z_hi * 2 + z_lo), core: 2. Of those that a mesh axis runs over, the one named last changes fastest.
Arguments:
- positions: float32 [3, 16384], P(None, 'blk'), may hold values from 0 to 256, as said below
- species: int32 [16384], P('blk'), may hold values from 0 to 1
- node_features: float32 [64, 16384], P('chan', 'blk'), may hold values from -6 to 6
- block_mask: int32 [128, 7], P('blk'), may hold values from 0 to 1, as said below
- radial_weight: float32 [8, 64], P(None, 'chan'), may hold values from -2 to 2
- species_embed: float32 [64, 2], P('chan'), may hold values from 0.25 to 1.75
- center_embed: float32 [64, 2], P('chan'), may hold values from 0.25 to 1.75
- mix_weight: float32 [3, 64, 64], replicated, may hold values from -0.75 to 0.75
Outputs:
- descriptors: float32 [3, 64, 16384], P(None, 'chan', 'blk')
Inputs may be any that keep to these rules, and one draw needn't show every extreme that they name: `positions`: atom g lies in slab s = g // 128: its first coordinate in [s * 5 / 3, (s + 1) * 5 / 3), the other two in [0, 48). An arbitrary set of kept slab pairs, symmetric between the two slabs of a pair: block_mask[i, 3 + k] equals block_mask[(i + k) mod 128, 3 - k]; the middle column is 1.
All inputs are finite; a program needn't handle non-finite values.
Results may differ from a plain program's by a relative error of at most 0.0035.
Values sent between devices are 32-bit elements; how exact they have to be, the bound alone decides.
A program may use at most 64 MiB of HBM per device.

v0:
```python
import math

import jax
import jax.numpy as jnp
from jax import lax
from jax.sharding import PartitionSpec as P

slab_width = 5.0 / 3.0
cross_width = 48.0
cut_radius = 5.0
soften = 0.25


def from_behind(value, axis, by):
    size = lax.axis_size(axis)
    return lax.ppermute(value, axis, [(i, (i + by) % size) for i in range(size)])


def cut_along(value, dim, size):
    before, after = (value.shape[:dim], value.shape[dim + 1 :])
    return jnp.moveaxis(value.reshape(*before, size, -1, *after), dim, 0)


def sum_at_owner(value, axis, dim):
    size = lax.axis_size(axis)
    parts = lax.all_to_all(cut_along(value, dim, size), axis, 0, 0, tiled=True)
    return jnp.sum(parts, axis=0)


def table_of(own_pos, other_pos, box_x, keep_pairs, count):
    separation = other_pos[:, None, :] - own_pos[:, :, None]
    lengths = jnp.array([box_x, cross_width, cross_width], dtype=jnp.float32)[:, None, None]
    separation = separation - lengths * jnp.floor(separation / lengths + 0.5)
    distance = jnp.sqrt(jnp.sum(separation * separation, axis=0) + soften)
    unit_x = separation[0] / distance
    unit_y = separation[1] / distance
    unit_z = separation[2] / distance
    root3 = math.sqrt(3.0)
    root15 = math.sqrt(15.0)
    harmonics = jnp.stack(
        [
            jnp.ones_like(distance),
            root3 * unit_x,
            root3 * unit_y,
            root3 * unit_z,
            root15 * unit_x * unit_y,
            root15 * unit_y * unit_z,
            0.5 * math.sqrt(5.0) * (2.0 * unit_z * unit_z - unit_x * unit_x - unit_y * unit_y),
            root15 * unit_x * unit_z,
            0.5 * root15 * (unit_x * unit_x - unit_y * unit_y),
        ]
    )
    scaled = distance / cut_radius
    polynomial = 1.0 - 28.0 * scaled**6 + 48.0 * scaled**7 - 21.0 * scaled**8
    envelope = jnp.where(scaled < 1.0, polynomial, 0.0) * keep_pairs
    orders = jnp.arange(1, count + 1, dtype=jnp.float32)[:, None, None]
    radial = (
        math.sqrt(2.0 / cut_radius)
        * jnp.sin(orders * (math.pi / cut_radius) * distance[None])
        / distance[None]
        * envelope[None]
    )
    return (radial[:, None] * harmonics[None]).astype(jnp.bfloat16)


def weights_lm(mix_weight):
    return jnp.concatenate(
        [
            mix_weight[0:1],
            jnp.repeat(mix_weight[1:2], 3, axis=0),
            jnp.repeat(mix_weight[2:3], 5, axis=0),
        ],
        axis=0,
    )


def describe(mixed_tensor):
    squares = mixed_tensor * mixed_tensor
    return jnp.log1p(
        jnp.stack(
            [squares[:, 0], jnp.sum(squares[:, 1:4], axis=1), jnp.sum(squares[:, 4:9], axis=1)]
        )
    )


def one_hot_of(species, kinds):
    return (species[None, :] == jnp.arange(kinds, dtype=jnp.int32)[:, None]).astype(jnp.float32)


def carried_of(species, node_features, species_embed, radial_weight):
    embedded = jnp.dot(
        species_embed, one_hot_of(species, species_embed.shape[1]), precision=lax.Precision.HIGHEST
    )
    return (radial_weight[:, :, None] * (node_features * embedded)[None]).astype(jnp.bfloat16)


def parity_signs():
    return jnp.array([1.0, -1.0, -1.0, -1.0, 1.0, 1.0, 1.0, 1.0, 1.0], dtype=jnp.float32)


def contributions(own_pos, own_carried, other_pos, other_carried, active, box_x, count):
    forward_shape = (other_carried.shape[1], 9, own_pos.shape[1])
    backward_shape = (own_carried.shape[1], 9, other_pos.shape[1])

    def compute():
        pair_table = table_of(own_pos, other_pos, box_x, active.astype(jnp.float32), count)
        forward = jnp.einsum(
            "ncb,nmab->cma", other_carried, pair_table, preferred_element_type=jnp.float32
        )
        backward = jnp.einsum(
            "nca,nmab->cmb", own_carried, pair_table, preferred_element_type=jnp.float32
        )
        return (forward, backward * parity_signs()[None, :, None])

    def skipped():
        return (jnp.zeros(forward_shape, jnp.float32), jnp.zeros(backward_shape, jnp.float32))

    return lax.cond(active > 0, compute, skipped)


def step_ahead(bundle):
    return from_behind(bundle, "blk", -1)


def shards(
    positions,
    species,
    node_features,
    block_mask,
    radial_weight,
    species_embed,
    center_embed,
    mix_weight,
):
    box_x = float(lax.axis_size("blk")) * slab_width
    reach = (block_mask.shape[1] - 1) // 2
    count = radial_weight.shape[0]
    atom_count = positions.shape[1]
    feats_all, spec_all, cent_all, radial_all = (
        node_features,
        species_embed,
        center_embed,
        radial_weight,
    )
    centre_rows = jnp.arange(atom_count, dtype=jnp.int32)
    no_self = 1.0 - (
        centre_rows[:, None] == jnp.arange(atom_count, dtype=jnp.int32)[None, :]
    ).astype(jnp.float32)
    slab_carried = carried_of(species, feats_all, spec_all, radial_all)
    self_table = table_of(
        positions, positions, box_x, block_mask[0, reach].astype(jnp.float32) * no_self, count
    )
    summed = jnp.einsum(
        "ncb,nmab->cma", slab_carried, self_table, preferred_element_type=jnp.float32
    )
    ahead = (positions, species, feats_all)
    partials = []
    for offset in range(1, reach + 1):
        ahead = step_ahead(ahead)
        ahead_carried = carried_of(ahead[1], ahead[2], spec_all, radial_all)
        forward, backward = contributions(
            positions,
            slab_carried,
            ahead[0],
            ahead_carried,
            block_mask[0, reach + offset],
            box_x,
            count,
        )
        summed = summed + forward
        partials.append(backward)
    returned = jnp.zeros((summed.shape[0], 9, atom_count), jnp.float32)
    for offset in range(reach, 0, -1):
        returned = from_behind(returned + partials[offset - 1], "blk", 1)
    summed = summed + returned
    centre = jnp.dot(
        cent_all, one_hot_of(species, cent_all.shape[1]), precision=lax.Precision.HIGHEST
    )
    features = summed * centre[:, None, :]
    weights_all = weights_lm(mix_weight)
    channel_count = features.shape[0]
    weights_in = lax.dynamic_slice_in_dim(
        weights_all, lax.axis_index("chan") * channel_count, channel_count, 2
    )
    mixed_tensor = sum_at_owner(
        jnp.einsum("mpc,cma->pma", weights_in, features, precision=lax.Precision.HIGHEST), "chan", 0
    )
    return describe(mixed_tensor)


def solution(mesh):
    return jax.shard_map(
        shards,
        mesh=mesh,
        in_specs=(
            P(None, "blk"),
            P("blk"),
            P("chan", "blk"),
            P("blk", None),
            P(None, "chan"),
            P("chan", None),
            P("chan", None),
            P(),
        ),
        out_specs=P(None, "chan", "blk"),
        check_vma=False,
    )
```

profile of v0, /device:TPU:1, one launch (start us, length us, event | category | flops | bytes accessed | tf_op | source)
XLA Modules:
  0.0 117.8 jit_solution(10155094599847018535)
XLA Ops:
  0.0 16.7 %collective-permute-start.1 = (f32[16,128]{1,0:T(8,128)}, f32[16,128]{1,0:T(8,128)S(1)}, u32[]{:S(2)}, u32[]{:S(2)}) collective-permute-start(f32[16,128]{1,0:T(8,128)} %param.23), channel_id=1, source_target_pairs={{0,508},{4,0},{8,4},{12,8},{16,12},{20,16},{24,20},{28,24},{32,28}... | collective-permute-start | bytes 24584 | tf_op jit(solution)/shard_map/ppermute | solution.py:16
  16.7 3.0 %collective-permute-start.2 = (s32[128]{0:T(128)}, s32[128]{0:T(128)S(1)}, u32[]{:S(2)}, u32[]{:S(2)}) collective-permute-start(s32[128]{0:T(128)} %param.22), channel_id=1, source_target_pairs={{0,508},{4,0},{8,4},{12,8},{16,12},{20,16},{24,20},{28,24},{32,28}... | collective-permute-start | bytes 1544 | tf_op jit(solution)/shard_map/ppermute | solution.py:16
  19.7 3.0 %collective-permute-start = (f32[3,128]{1,0:T(4,128)}, f32[3,128]{1,0:T(4,128)S(1)}, u32[]{:S(2)}, u32[]{:S(2)}) collective-permute-start(f32[3,128]{1,0:T(4,128)} %param.21), channel_id=1, source_target_pairs={{0,508},{4,0},{8,4},{12,8},{16,12},{20,16},{24,20},{28,24},{32,28}... | collective-permute-start | bytes 4616 | tf_op jit(solution)/shard_map/ppermute | solution.py:16
  22.7 0.9 multiply_reduce_fusion.3
  23.7 0.0 copy-start.4
  23.8 0.1 fusion.130
  23.9 0.4 copy-done.4
  24.4 0.7 fusion.152
  25.7 0.1 add_sqrt_fusion.3
  25.8 0.0 copy-start.5
  25.8 0.0 copy-start.2
  25.8 0.0 copy-start.3
  25.8 0.0 copy-start.9
  25.8 1.8 %divide_multiply_fusion.3 = f32[8,128,128]{2,1,0:T(8,128)S(1)} fusion(f32[128,128]{1,0:T(8,128)S(1)} %get-tuple-element.108, f32[128,128]{1,0:T(8,128)S(1)} %get-tuple-element.107, f32[8]{0:T(128)S(1)} %add_multiply_fusion.3), kind=kLoop, calls=%fused_computation.185 | loop fusion | flops 524288 | bytes 655392 | tf_op jit(solution)/shard_map/mul | solution.py:58
  27.6 3.0 %collective-permute-start.5 = (s32[128]{0:T(128)S(1)}, s32[128]{0:T(128)S(1)}, u32[]{:S(2)}, u32[]{:S(2)}) collective-permute-start(s32[128]{0:T(128)S(1)} %collective-permute-done.2), channel_id=1, source_target_pairs={{0,508},{4,0},{8,4},{12,8},{16,12},{20,16},{24,20},{28,24},{32,28}... | collective-permute-start | bytes 1544 | tf_op jit(solution)/shard_map/ppermute | solution.py:16
  30.6 2.9 %collective-permute-start.3 = (f32[3,128]{1,0:T(4,128)S(1)}, f32[3,128]{1,0:T(4,128)S(1)}, u32[]{:S(2)}, u32[]{:S(2)}) collective-permute-start(f32[3,128]{1,0:T(4,128)S(1)} %collective-permute-done), channel_id=1, source_target_pairs={{0,508},{4,0},{8,4},{12,8},{16,12},{20,16},{24,20},{28,24},{32,28}... | collective-permute-start | bytes 4616 | tf_op jit(solution)/shard_map/ppermute | solution.py:16
  33.6 0.2 fusion.106
  34.4 6.8 %collective-permute-start.8 = (s32[128]{0:T(128)S(1)}, s32[128]{0:T(128)S(1)}, u32[]{:S(2)}, u32[]{:S(2)}) collective-permute-start(s32[128]{0:T(128)S(1)} %collective-permute-done.5), channel_id=1, source_target_pairs={{0,508},{4,0},{8,4},{12,8},{16,12},{20,16},{24,20},{28,24},{32,28}... | collective-permute-start | bytes 1544 | tf_op jit(solution)/shard_map/ppermute | solution.py:16
  41.3 2.9 %collective-permute-start.6 = (f32[3,128]{1,0:T(4,128)S(1)}, f32[3,128]{1,0:T(4,128)S(1)}, u32[]{:S(2)}, u32[]{:S(2)}) collective-permute-start(f32[3,128]{1,0:T(4,128)S(1)} %collective-permute-done.3), channel_id=1, source_target_pairs={{0,508},{4,0},{8,4},{12,8},{16,12},{20,16},{24,20},{28,24},{32,28}... | collective-permute-start | bytes 4616 | tf_op jit(solution)/shard_map/ppermute | solution.py:16
  44.2 1.9 %collective-permute-start.4 = (f32[16,128]{1,0:T(8,128)S(1)}, f32[16,128]{1,0:T(8,128)S(1)}, u32[]{:S(2)}, u32[]{:S(2)}) collective-permute-start(f32[16,128]{1,0:T(8,128)S(1)} %collective-permute-done.1), channel_id=1, source_target_pairs={{0,508},{4,0},{8,4},{12,8},{16,12},{20,16},{24,20},{28,24},{32,28}... | collective-permute-start | bytes 24584 | tf_op jit(solution)/shard_map/ppermute | solution.py:16
  46.1 0.2 fusion.105
  46.3 2.3 %collective-permute-done.4 = f32[16,128]{1,0:T(8,128)S(1)} collective-permute-done((f32[16,128]{1,0:T(8,128)S(1)}, f32[16,128]{1,0:T(8,128)S(1)}, u32[]{:S(2)}, u32[]{:S(2)}) %collective-permute-start.4) | collective-permute-done | bytes 8224 | tf_op jit(solution)/shard_map/ppermute | solution.py:16
  48.6 8.2 %collective-permute-start.7 = (f32[16,128]{1,0:T(8,128)S(1)}, f32[16,128]{1,0:T(8,128)S(1)}, u32[]{:S(2)}, u32[]{:S(2)}) collective-permute-start(f32[16,128]{1,0:T(8,128)S(1)} %collective-permute-done.4), channel_id=1, source_target_pairs={{0,508},{4,0},{8,4},{12,8},{16,12},{20,16},{24,20},{28,24},{32,28}... | collective-permute-start | bytes 24584 | tf_op jit(solution)/shard_map/ppermute | solution.py:16
  56.8 0.2 fusion.104
  57.0 0.6 collective-permute-done.7
  57.6 0.2 fusion.103
  57.8 0.1 multiply_convert_fusion.39
  57.9 0.0 copy-start.1
  58.0 4.2 %conditional.5 = (f32[16,9,128]{2,0,1:T(8,128)S(1)}, f32[16,9,128]{2,0,1:T(8,128)S(1)}) conditional(s32[]{:T(128)} %convert_element_type.69, () %tuple.33, (f32[3,128]{1,0:T(4,128)S(1)}, f32[3,128]{1,0:T(4,128)S(1)}, f32[3]{0:T(128)S(1)}, s32[]{:T(128)}, bf16[8,16,128]{2,1,0:T(8,128)(2,1)S(1)}, /*index=5*/bf16[8,16,128]{2,1,0:T(8,128)(2,1)S(1)}, ...), branch_computations={%region_7.8_spmd, %region_8.10_spmd} | conditional | flops 81987600 | bytes 5655692 | solution.py:118
  58.0 0.1 multiply_reduce_fusion.2
  58.3 0.1 fusion.90
  59.1 0.1 add_sqrt_fusion.2
  59.1 1.8 %divide_multiply_fusion.2 = f32[8,128,128]{2,1,0:T(8,128)S(1)} fusion(f32[128,128]{1,0:T(8,128)S(1)} %get-tuple-element.101, f32[128,128]{1,0:T(8,128)S(1)} %get-tuple-element.100, f32[8]{0:T(128)S(1)} %add_multiply_fusion.2), kind=kLoop, calls=%fused_computation.125 | loop fusion | flops 524288 | bytes 655392 | tf_op jit(solution)/shard_map/cond/branch_1_fun/mul | solution.py:58
  60.9 0.4 fusion.75
  61.4 0.7 fusion.72
  62.1 1.9 %collective-permute-start.9 = (f32[16,9,128]{2,0,1:T(8,128)S(1)}, f32[16,9,128]{2,0,1:T(8,128)S(1)}, u32[]{:S(2)}, u32[]{:S(2)}) collective-permute-start(f32[16,9,128]{2,0,1:T(8,128)S(1)} %get-tuple-element.77), channel_id=1, source_target_pairs={{0,4},{4,8},{8,12},{12,16},{16,20},{20,24},{24,28},{28,32},{32,36}... | collective-permute-start | bytes 221192 | tf_op jit(solution)/shard_map/ppermute | solution.py:16
  64.7 0.0 copy-start.7
  64.7 4.2 %conditional.4 = (f32[16,9,128]{2,0,1:T(8,128)S(1)}, f32[16,9,128]{2,0,1:T(8,128)S(1)}) conditional(s32[]{:T(128)} %convert_element_type.67, () %tuple.31, (f32[3,128]{1,0:T(4,128)S(1)}, f32[3,128]{1,0:T(4,128)S(1)}, f32[3]{0:T(128)S(1)}, s32[]{:T(128)}, bf16[8,16,128]{2,1,0:T(8,128)(2,1)S(1)}, /*index=5*/bf16[8,16,128]{2,1,0:T(8,128)(2,1)S(1)}, ...), branch_computations={%region_4.5_spmd, %region_5.7_spmd} | conditional | flops 81987600 | bytes 5655692 | solution.py:118
  64.7 0.1 multiply_reduce_fusion.1
  65.1 0.1 fusion.57
  65.8 0.1 add_sqrt_fusion.1
  65.9 1.8 %divide_multiply_fusion.1 = f32[8,128,128]{2,1,0:T(8,128)S(1)} fusion(f32[128,128]{1,0:T(8,128)S(1)} %get-tuple-element.97, f32[128,128]{1,0:T(8,128)S(1)} %get-tuple-element.96, f32[8]{0:T(128)S(1)} %add_multiply_fusion.1), kind=kLoop, calls=%fused_computation.68 | loop fusion | flops 524288 | bytes 655392 | tf_op jit(solution)/shard_map/cond/branch_1_fun/mul | solution.py:58
  67.7 0.4 fusion.42
  68.2 0.7 fusion.39
  68.9 5.7 %collective-permute-done.9 = f32[16,9,128]{2,0,1:T(8,128)S(1)} collective-permute-done((f32[16,9,128]{2,0,1:T(8,128)S(1)}, f32[16,9,128]{2,0,1:T(8,128)S(1)}, u32[]{:S(2)}, u32[]{:S(2)}) %collective-permute-start.9) | collective-permute-done | bytes 73760 | tf_op jit(solution)/shard_map/ppermute | solution.py:16
  74.6 1.9 %collective-permute-start.10 = (f32[16,9,128]{2,0,1:T(8,128)S(1)}, f32[16,9,128]{2,0,1:T(8,128)S(1)}, u32[]{:S(2)}, u32[]{:S(2)}) collective-permute-start(f32[16,9,128]{2,0,1:T(8,128)S(1)} %add.200), channel_id=1, source_target_pairs={{0,4},{4,8},{8,12},{12,16},{16,20},{20,24},{24,28},{28,32},{32,36}... | collective-permute-start | bytes 221192 | tf_op jit(solution)/shard_map/ppermute | solution.py:16
  76.5 0.2 convolution_bitcast_fusion
  77.4 4.4 %conditional.3 = (f32[16,9,128]{2,0,1:T(8,128)S(1)}, f32[16,9,128]{2,0,1:T(8,128)S(1)}) conditional(s32[]{:T(128)} %convert_element_type.65, () %tuple.29, (f32[3,128]{1,0:T(4,128)S(1)}, f32[3,128]{1,0:T(4,128)S(1)}, f32[3]{0:T(128)S(1)}, s32[]{:T(128)}, bf16[8,16,128]{2,1,0:T(8,128)(2,1)S(1)}, /*index=5*/bf16[8,16,128]{2,1,0:T(8,128)(2,1)S(1)}, ...), branch_computations={%region_1.2_spmd, %region_2.4_spmd} | conditional | flops 81987600 | bytes 5655692 | solution.py:118
  77.6 0.1 multiply_reduce_fusion
  77.9 0.1 fusion.24
  78.6 0.1 add_sqrt_fusion
  78.7 1.8 %divide_multiply_fusion = f32[8,128,128]{2,1,0:T(8,128)S(1)} fusion(f32[128,128]{1,0:T(8,128)S(1)} %get-tuple-element.93, f32[128,128]{1,0:T(8,128)S(1)} %get-tuple-element.92, f32[8]{0:T(128)S(1)} %add_multiply_fusion), kind=kLoop, calls=%fused_computation.11 | loop fusion | flops 524288 | bytes 655392 | tf_op jit(solution)/shard_map/cond/branch_1_fun/mul | solution.py:58
  80.5 0.4 fusion.9
  81.0 0.7 fusion.6
  81.7 5.1 %collective-permute-done.10 = f32[16,9,128]{2,0,1:T(8,128)S(1)} collective-permute-done((f32[16,9,128]{2,0,1:T(8,128)S(1)}, f32[16,9,128]{2,0,1:T(8,128)S(1)}, u32[]{:S(2)}, u32[]{:S(2)}) %collective-permute-start.10) | collective-permute-done | bytes 73760 | tf_op jit(solution)/shard_map/ppermute | solution.py:16
  86.8 1.9 %collective-permute-start.11 = (f32[16,9,128]{2,0,1:T(8,128)S(1)}, f32[16,9,128]{2,0,1:T(8,128)S(1)}, u32[]{:S(2)}, u32[]{:S(2)}) collective-permute-start(f32[16,9,128]{2,0,1:T(8,128)S(1)} %add.201), channel_id=1, source_target_pairs={{0,4},{4,8},{8,12},{12,16},{16,20},{20,24},{24,28},{28,32},{32,36}... | collective-permute-start | bytes 221192 | tf_op jit(solution)/shard_map/ppermute | solution.py:16
  88.7 0.7 fusion.102
  89.5 0.1 copy.25
  89.5 0.1 copy.24
  89.6 0.1 copy.34
  89.7 9.3 %collective-permute-done.11 = f32[16,9,128]{2,0,1:T(8,128)S(1)} collective-permute-done((f32[16,9,128]{2,0,1:T(8,128)S(1)}, f32[16,9,128]{2,0,1:T(8,128)S(1)}, u32[]{:S(2)}, u32[]{:S(2)}) %collective-permute-start.11) | collective-permute-done | bytes 73760 | tf_op jit(solution)/shard_map/ppermute | solution.py:16
  99.0 0.7 fusion.112
  99.7 17.4 %all_to_all.5 = f32[4,16,9,128]{3,1,2,0:T(8,128)S(1)} all-to-all(f32[4,16,9,128]{3,1,2,0:T(8,128)S(1)} %copy.26), channel_id=1, replica_groups=mesh['blk'=128,'chan'=4] {'chan'}, dimensions={0} | all-to-all | bytes 589824 | tf_op jit(solution)/shard_map/all_to_all | solution.py:26
  117.1 0.6 maximum_log-plus-one_fusion
  (66 shorter events, 1.0 us)
Async XLA Ops:
  0.0 33.5 %copy-start = (f32[16,2]{0,1:T(2,128)S(1)}, f32[16,2]{0,1:T(2,128)}, u32[]{:S(2)}) copy-start(f32[16,2]{0,1:T(2,128)} %param.26) | copy-start | bytes 388
  0.0 44.2 %collective-permute-start.1 = (f32[16,128]{1,0:T(8,128)}, f32[16,128]{1,0:T(8,128)S(1)}, u32[]{:S(2)}, u32[]{:S(2)}) collective-permute-start(f32[16,128]{1,0:T(8,128)} %param.23), channel_id=1, source_target_pairs={{0,508},{4,0},{8,4},{12,8},{16,12},{20,16},{24,20},{28,24},{32,28}... | collective-permute-start | bytes 24584 | tf_op jit(solution)/shard_map/ppermute | solution.py:16
  16.7 10.9 %collective-permute-start.2 = (s32[128]{0:T(128)}, s32[128]{0:T(128)S(1)}, u32[]{:S(2)}, u32[]{:S(2)}) collective-permute-start(s32[128]{0:T(128)} %param.22), channel_id=1, source_target_pairs={{0,508},{4,0},{8,4},{12,8},{16,12},{20,16},{24,20},{28,24},{32,28}... | collective-permute-start | bytes 1544 | tf_op jit(solution)/shard_map/ppermute | solution.py:16
  19.7 10.9 %collective-permute-start = (f32[3,128]{1,0:T(4,128)}, f32[3,128]{1,0:T(4,128)S(1)}, u32[]{:S(2)}, u32[]{:S(2)}) collective-permute-start(f32[3,128]{1,0:T(4,128)} %param.21), channel_id=1, source_target_pairs={{0,508},{4,0},{8,4},{12,8},{16,12},{20,16},{24,20},{28,24},{32,28}... | collective-permute-start | bytes 4616 | tf_op jit(solution)/shard_map/ppermute | solution.py:16
  23.7 0.7 copy-start.4
  24.4 9.2 %copy-start.6 = (f32[16,128]{1,0:T(8,128)S(1)}, f32[16,128]{1,0:T(8,128)}, u32[]{:S(2)}) copy-start(f32[16,128]{1,0:T(8,128)} %param.23) | copy-start | bytes 24580
  24.4 9.2 %copy-start.8 = (s32[128]{0:T(128)S(1)}, s32[128]{0:T(128)}, u32[]{:S(2)}) copy-start(s32[128]{0:T(128)} %param.22) | copy-start | bytes 1540
  25.8 32.0 %copy-start.5 = (f32[8,16]{1,0:T(8,128)S(1)}, f32[8,16]{1,0:T(8,128)}, u32[]{:S(2)}) copy-start(f32[8,16]{1,0:T(8,128)} %param.25) | copy-start | bytes 1540
  25.8 32.2 %copy-start.2 = (f32[3,128]{1,0:T(4,128)S(1)}, f32[3,128]{1,0:T(4,128)}, u32[]{:S(2)}) copy-start(f32[3,128]{1,0:T(4,128)} %param.21) | copy-start | bytes 4612
  25.8 32.1 %copy-start.3 = (f32[3]{0:T(128)S(1)}, f32[3]{0:T(128)}, u32[]{:S(2)}) copy-start(f32[3]{0:T(128)} %constant.66.clone) | copy-start | bytes 40
  25.8 32.1 %copy-start.9 = (f32[9]{0:T(128)S(1)}, f32[9]{0:T(128)}, u32[]{:S(2)}) copy-start(f32[9]{0:T(128)} %constant.96.clone) | copy-start | bytes 112
  27.6 6.8 %collective-permute-start.5 = (s32[128]{0:T(128)S(1)}, s32[128]{0:T(128)S(1)}, u32[]{:S(2)}, u32[]{:S(2)}) collective-permute-start(s32[128]{0:T(128)S(1)} %collective-permute-done.2), channel_id=1, source_target_pairs={{0,508},{4,0},{8,4},{12,8},{16,12},{20,16},{24,20},{28,24},{32,28}... | collective-permute-start | bytes 1544 | tf_op jit(solution)/shard_map/ppermute | solution.py:16
  30.6 10.6 %collective-permute-start.3 = (f32[3,128]{1,0:T(4,128)S(1)}, f32[3,128]{1,0:T(4,128)S(1)}, u32[]{:S(2)}, u32[]{:S(2)}) collective-permute-start(f32[3,128]{1,0:T(4,128)S(1)} %collective-permute-done), channel_id=1, source_target_pairs={{0,508},{4,0},{8,4},{12,8},{16,12},{20,16},{24,20},{28,24},{32,28}... | collective-permute-start | bytes 4616 | tf_op jit(solution)/shard_map/ppermute | solution.py:16
  34.4 22.6 %collective-permute-start.8 = (s32[128]{0:T(128)S(1)}, s32[128]{0:T(128)S(1)}, u32[]{:S(2)}, u32[]{:S(2)}) collective-permute-start(s32[128]{0:T(128)S(1)} %collective-permute-done.5), channel_id=1, source_target_pairs={{0,508},{4,0},{8,4},{12,8},{16,12},{20,16},{24,20},{28,24},{32,28}... | collective-permute-start | bytes 1544 | tf_op jit(solution)/shard_map/ppermute | solution.py:16
  41.3 16.6 %collective-permute-start.6 = (f32[3,128]{1,0:T(4,128)S(1)}, f32[3,128]{1,0:T(4,128)S(1)}, u32[]{:S(2)}, u32[]{:S(2)}) collective-permute-start(f32[3,128]{1,0:T(4,128)S(1)} %collective-permute-done.3), channel_id=1, source_target_pairs={{0,508},{4,0},{8,4},{12,8},{16,12},{20,16},{24,20},{28,24},{32,28}... | collective-permute-start | bytes 4616 | tf_op jit(solution)/shard_map/ppermute | solution.py:16
  44.2 4.4 %collective-permute-start.4 = (f32[16,128]{1,0:T(8,128)S(1)}, f32[16,128]{1,0:T(8,128)S(1)}, u32[]{:S(2)}, u32[]{:S(2)}) collective-permute-start(f32[16,128]{1,0:T(8,128)S(1)} %collective-permute-done.1), channel_id=1, source_target_pairs={{0,508},{4,0},{8,4},{12,8},{16,12},{20,16},{24,20},{28,24},{32,28}... | collective-permute-start | bytes 24584 | tf_op jit(solution)/shard_map/ppermute | solution.py:16
  48.6 9.0 %collective-permute-start.7 = (f32[16,128]{1,0:T(8,128)S(1)}, f32[16,128]{1,0:T(8,128)S(1)}, u32[]{:S(2)}, u32[]{:S(2)}) collective-permute-start(f32[16,128]{1,0:T(8,128)S(1)} %collective-permute-done.4), channel_id=1, source_target_pairs={{0,508},{4,0},{8,4},{12,8},{16,12},{20,16},{24,20},{28,24},{32,28}... | collective-permute-start | bytes 24584 | tf_op jit(solution)/shard_map/ppermute | solution.py:16
  57.9 6.1 %copy-start.1 = (f32[3,64,64]{2,1,0:T(8,128)S(1)}, f32[3,64,64]{2,1,0:T(8,128)}, u32[]{:S(2)}) copy-start(f32[3,64,64]{2,1,0:T(8,128)} %param.28) | copy-start | bytes 147460
  62.1 12.4 %collective-permute-start.9 = (f32[16,9,128]{2,0,1:T(8,128)S(1)}, f32[16,9,128]{2,0,1:T(8,128)S(1)}, u32[]{:S(2)}, u32[]{:S(2)}) collective-permute-start(f32[16,9,128]{2,0,1:T(8,128)S(1)} %get-tuple-element.77), channel_id=1, source_target_pairs={{0,4},{4,8},{8,12},{12,16},{16,20},{20,24},{24,28},{28,32},{32,36}... | collective-permute-start | bytes 221192 | tf_op jit(solution)/shard_map/ppermute | solution.py:16
  64.7 11.8 %copy-start.7 = (f32[16,2]{0,1:T(2,128)S(1)}, f32[16,2]{0,1:T(2,128)}, u32[]{:S(2)}) copy-start(f32[16,2]{0,1:T(2,128)} %param.27) | copy-start | bytes 388
  74.6 12.2 %collective-permute-start.10 = (f32[16,9,128]{2,0,1:T(8,128)S(1)}, f32[16,9,128]{2,0,1:T(8,128)S(1)}, u32[]{:S(2)}, u32[]{:S(2)}) collective-permute-start(f32[16,9,128]{2,0,1:T(8,128)S(1)} %add.200), channel_id=1, source_target_pairs={{0,4},{4,8},{8,12},{12,16},{16,20},{20,24},{24,28},{28,32},{32,36}... | collective-permute-start | bytes 221192 | tf_op jit(solution)/shard_map/ppermute | solution.py:16
  86.8 12.2 %collective-permute-start.11 = (f32[16,9,128]{2,0,1:T(8,128)S(1)}, f32[16,9,128]{2,0,1:T(8,128)S(1)}, u32[]{:S(2)}, u32[]{:S(2)}) collective-permute-start(f32[16,9,128]{2,0,1:T(8,128)S(1)} %add.201), channel_id=1, source_target_pairs={{0,4},{4,8},{8,12},{12,16},{16,20},{20,24},{24,28},{28,32},{32,36}... | collective-permute-start | bytes 221192 | tf_op jit(solution)/shard_map/ppermute | solution.py:16
where the time goes:
time: 118 us
  starting transfers between devices  54.2 us (46%)
  waiting for transfers between devices  22.9 us (19%)
  blocking collectives  17.4 us (15%)
  other arithmetic  10.6 us (9%)
  matrix products  5.89 us (5%)
  between operations  3.01 us (3%)
  loops' own time  2.37 us (2%)
  local copies, waits for them, and re-layouts  1.48 us (1%)
    ppermute x12, starting transfers between devices, from_behind(): lax.ppermute(value, axis, [(i, (i + by) % size) for i in range(size)])  54.2 us
    ppermute x12, waiting for transfers between devices, from_behind(): lax.ppermute(value, axis, [(i, (i + by) % size) for i in range(size)])  22.9 us
    all_to_all x1, blocking collectives, sum_at_owner(): parts = lax.all_to_all(cut_along(value, dim, size), axis, 0, 0, tiled=True)  17.4 us
    mul x4, other arithmetic, table_of(): math.sqrt(2.0 / cut_radius)  7.22 us
    another operation x3, loops' own time, contributions(): return lax.cond(active > 0, compute, skipped)  2.37 us
  transfers between devices with their start and end apart: 12, of which 5 were waited for; matrix products, arithmetic and copies ran while one was open for 11% of the time, Pallas kernels for 0%

commit v1 on v0

v1 whole, which is shorter than its diff:
```python
import functools
import math

import jax
import jax.numpy as jnp
from jax import lax
from jax.experimental import pallas as pl
from jax.experimental.pallas import tpu as pltpu
from jax.sharding import PartitionSpec as P

MESH = pl.DeviceIdType.MESH

slab_width = 5.0 / 3.0
cross_width = 48.0
cut_radius = 5.0
soften = 0.25

HOPS = 3
ATOMS = 128
CHANS = 4
CD = 16
C = 64
NB = 8
NM = 9
HALF = 16
BF = jnp.bfloat16
F32 = jnp.float32


def sin_cos(angle):
    x = angle - 0.5 * math.pi
    y = x * x
    even = 2.0876756987868099e-9 * y - 2.755731922398589e-7
    even = even * y + 2.48015873015873e-5
    even = even * y - 1.388888888888889e-3
    even = even * y + 4.1666666666666664e-2
    even = even * y - 0.5
    even = even * y + 1.0
    odd = -2.505210838544172e-8 * y + 2.7557319223985893e-6
    odd = odd * y - 1.984126984126984e-4
    odd = odd * y + 8.333333333333333e-3
    odd = odd * y - 1.6666666666666666e-1
    odd = odd * y * x + x
    return even, -odd


def kernel(
    box_x,
    n_blk,
    pos_hbm,
    spe_hbm,
    fea_hbm,
    msk_hbm,
    rad_hbm,
    sem_hbm,
    cem_hbm,
    mix_hbm,
    out_ref,
    pos,
    spe,
    fea,
    msk,
    rad,
    emb,
    cen,
    mix,
    maskb,
    radb,
    embb,
    tab,
    carr,
    acc,
    lsem,
    fs,
    fr,
    ps,
    pr,
    ss,
    sr,
    gs,
    gr,
    qs,
    qr,
):
    me = lax.axis_index("blk")
    ch = lax.axis_index("chan")
    last = n_blk - HOPS
    late = me >= last
    partner = ch + 1 - 2 * lax.rem(ch, 2)

    def slab(offset):
        return lax.rem(me + offset + n_blk, n_blk)

    def chan(c):
        return lax.rem(ch + c, CHANS)

    def to(offset, c):
        return {"blk": slab(offset), "chan": chan(c)}

    barrier = pltpu.get_barrier_semaphore()

    def greet(offset, c):
        pl.semaphore_signal(barrier, inc=1, device_id=to(offset, c), device_id_type=MESH)

    for c in (1, 2, 3):
        greet(0, c)
    for k in (1, 2, 3):
        greet(-k, 0)
        greet(-k, 2)
    for k in (1, 2, 3):

        @pl.when(me + k < last)
        def _(k=k):
            greet(k, 0)
            greet(k, 2)

    first = [
        pltpu.make_async_copy(pos_hbm, pos.at[HOPS], lsem.at[0]),
        pltpu.make_async_copy(spe_hbm, spe.at[HOPS], lsem.at[1]),
        pltpu.make_async_copy(fea_hbm, fea.at[HOPS, ch], lsem.at[2]),
    ]
    params = [
        pltpu.make_async_copy(rad_hbm, rad.at[ch], lsem.at[3]),
        pltpu.make_async_copy(sem_hbm, emb.at[ch], lsem.at[4]),
        pltpu.make_async_copy(cem_hbm, cen.at[ch], lsem.at[5]),
    ]
    rest = [
        pltpu.make_async_copy(msk_hbm, msk, lsem.at[6]),
        pltpu.make_async_copy(
            mix_hbm.at[:, pl.ds(pl.multiple_of(ch * CD, CD), CD), :], mix, lsem.at[7]
        ),
    ]
    for copy in first + params + rest:
        copy.start()
    for copy in first:
        copy.wait()
    lower = jnp.where(late, 0, jnp.minimum(me, HOPS))
    pl.semaphore_wait(barrier, 3 + 2 * (HOPS + lower))

    def sends(offset):
        slot = HOPS - offset
        out = []
        for c in (0, 2):
            out.append(
                pltpu.make_async_remote_copy(
                    src_ref=fea.at[HOPS, ch],
                    dst_ref=fea.at[slot, ch],
                    send_sem=fs.at[slot, c],
                    recv_sem=fr.at[slot, ch],
                    device_id=to(offset, c),
                    device_id_type=MESH,
                )
            )
        out.append(
            pltpu.make_async_remote_copy(
                src_ref=pos.at[HOPS],
                dst_ref=pos.at[slot],
                send_sem=ps.at[slot],
                recv_sem=pr.at[slot],
                device_id=to(offset, 0),
                device_id_type=MESH,
            )
        )
        out.append(
            pltpu.make_async_remote_copy(
                src_ref=spe.at[HOPS],
                dst_ref=spe.at[slot],
                send_sem=ss.at[slot],
                recv_sem=sr.at[slot],
                device_id=to(offset, 0),
                device_id_type=MESH,
            )
        )
        return out

    for k in (3, 2, 1):
        for copy in sends(k):
            copy.start()
    for k in (1, 2, 3):

        @pl.when(jnp.logical_and(me < last, me >= k))
        def _(k=k):
            for copy in sends(-k):
                copy.start()

    for copy in params:
        copy.wait()
    gathers = []
    for c in (1, 2, 3):
        for q, (ref, sem, got) in enumerate(
            (
                (rad.at[ch], qs.at[0, c], qr.at[0, ch]),
                (emb.at[ch], qs.at[1, c], qr.at[1, ch]),
                (cen.at[ch], qs.at[2, c], qr.at[2, ch]),
                (fea.at[HOPS, ch], gs.at[HOPS, c], gr.at[HOPS, ch]),
            )
        ):
            gathers.append(
                pltpu.make_async_remote_copy(
                    src_ref=ref,
                    dst_ref=ref,
                    send_sem=sem,
                    recv_sem=got,
                    device_id=to(0, c),
                    device_id_type=MESH,
                )
            )
    for copy in gathers:
        copy.start()

    def relays(slot):
        out = []
        for q, c in ((0, 0), (1, 2)):
            a = chan(c)
            out.append(
                pltpu.make_async_remote_copy(
                    src_ref=fea.at[slot, a],
                    dst_ref=fea.at[slot, a],
                    send_sem=gs.at[slot, q],
                    recv_sem=gr.at[slot, a],
                    device_id={"blk": me, "chan": partner},
                    device_id_type=MESH,
                )
            )
        return out

    def arrived(ref, sem):
        pltpu.make_async_remote_copy(
            src_ref=ref,
            dst_ref=ref,
            send_sem=lsem.at[8],
            recv_sem=sem,
            device_id={"blk": me, "chan": partner},
            device_id_type=MESH,
        ).wait_recv()

    for copy in rest:
        copy.wait()
    for s in range(2 * HOPS + 1):
        maskb[s] = jnp.broadcast_to(msk[:, s : s + 1].astype(F32), (8, ATOMS))

    for c in (1, 2, 3):
        a = chan(c)
        arrived(rad.at[a], qr.at[0, a])
        arrived(emb.at[a], qr.at[1, a])
        arrived(cen.at[a], qr.at[2, a])
        arrived(fea.at[HOPS, a], gr.at[HOPS, a])

    eye = lax.broadcasted_iota(jnp.int32, (CD, CD), 0) == lax.broadcasted_iota(
        jnp.int32, (CD, CD), 1
    )
    for q in range(CHANS):
        rows = slice(q * CD, (q + 1) * CD)
        for n in range(NB):
            row = jnp.broadcast_to(rad[q, n : n + 1, :], (CD, CD))
            column = jnp.sum(jnp.where(eye, row, 0.0), axis=1, keepdims=True)
            radb[n, rows, :] = jnp.broadcast_to(column, (CD, ATOMS))
        for kind in (0, 1):
            for at, ref in ((kind, emb), (2 + kind, cen)):
                row = jnp.broadcast_to(ref[q, kind : kind + 1, :], (CD, CD))
                column = jnp.sum(jnp.where(eye, row, 0.0), axis=1, keepdims=True)
                embb[at, rows, :] = jnp.broadcast_to(column, (CD, ATOMS))

    acc[...] = jnp.zeros_like(acc)
    own = pos[HOPS]
    own_x, own_y, own_z = own[0:1], own[1:2], own[2:3]
    lane = lax.broadcasted_iota(jnp.int32, (HALF, ATOMS), 1)
    sublane = lax.broadcasted_iota(jnp.int32, (HALF, ATOMS), 0)
    root3 = math.sqrt(3.0)
    ratio = math.sqrt(5.0 / 3.0)

    def offset_at(t):
        k = lax.rem(t + 2, 3) + 1
        sign = jnp.where(late, -1, 1) * jnp.where(t <= 3, 1, -1)
        return jnp.where(t == 0, 0, sign * k)

    def fetch(t):
        offset = offset_at(t)
        slot = offset + HOPS
        arrived(pos.at[slot], pr.at[slot])
        arrived(spe.at[slot], sr.at[slot])
        for c in (0, 2):
            a = chan(c)
            arrived(fea.at[slot, a], fr.at[slot, a])
        for copy in relays(slot):
            copy.start()
        k = lax.rem(t + 2, 3) + 1
        early = jnp.logical_and(me < last, me >= k)

        @pl.when(jnp.logical_and(offset < 0, jnp.logical_not(early)))
        def _():
            for copy in sends(offset):
                copy.start()

    def pairs(slot, apart):
        kinds = jnp.broadcast_to(spe[slot], (C, ATOMS)) == 1
        embedded = jnp.where(kinds, embb[1], embb[0])
        scaled = fea[slot].reshape(C, ATOMS) * embedded
        for n in range(NB):
            carr[:, n * ATOMS : (n + 1) * ATOMS] = (radb[n] * scaled).astype(BF)
        other = jnp.concatenate([pos[slot], jnp.zeros((5, ATOMS), F32)], axis=0)
        columns = jnp.transpose(other)
        keep = maskb[slot]
        keep = jnp.concatenate([keep, keep], axis=0)
        for tile in range(ATOMS // HALF):
            rows = slice(tile * HALF, (tile + 1) * HALF)
            dx = columns[rows, 0:1] - own_x
            dy = columns[rows, 1:2] - own_y
            dz = columns[rows, 2:3] - own_z
            dx = dx - box_x * jnp.floor(dx * (1.0 / box_x) + 0.5)
            dy = dy - cross_width * jnp.floor(dy * (1.0 / cross_width) + 0.5)
            dz = dz - cross_width * jnp.floor(dz * (1.0 / cross_width) + 0.5)
            square = dx * dx + dy * dy + dz * dz + soften
            inverse = lax.rsqrt(square)
            distance = square * inverse
            short = jnp.minimum(distance, cut_radius)
            x = short * (1.0 / cut_radius)
            x2 = x * x
            inner = x * (48.0 - 21.0 * x) - 28.0
            envelope = jnp.where(distance < cut_radius, 1.0 + x2 * x2 * x2 * inner, 0.0)
            same = (sublane + tile * HALF) == (lane + apart)
            amplitude = jnp.where(
                same, 0.0, (math.sqrt(2.0 / cut_radius) * inverse) * (envelope * keep)
            )
            sine, cosine = sin_cos(short * (math.pi / cut_radius))
            twice = 2.0 * cosine
            radial = [amplitude * sine]
            radial.append(twice * radial[0])
            for n in range(2, NB):
                radial.append(twice * radial[n - 1] - radial[n - 2])
            scale = inverse * root3
            hx, hy, hz = dx * scale, dy * scale, dz * scale
            gx, gy = ratio * hx, ratio * hy
            xx, yy = gx * hx, gy * hy
            zz = (2.0 * ratio) * (hz * hz)
            harmonics = [
                None,
                hx,
                hy,
                hz,
                gx * hy,
                gy * hz,
                (0.5 / root3) * (zz - xx - yy),
                gx * hz,
                0.5 * (xx - yy),
            ]
            for n in range(NB):
                at = slice(n * ATOMS + tile * HALF, n * ATOMS + (tile + 1) * HALF)
                for m in range(NM):
                    value = radial[n] if m == 0 else radial[n] * harmonics[m]
                    tab[at, m * ATOMS : (m + 1) * ATOMS] = value.astype(BF)
        acc[...] += jnp.dot(carr[...], tab[...], preferred_element_type=F32)

    def step(t, carry):
        @pl.when(t < 2 * HOPS)
        def _():
            fetch(t + 1)

        slot = offset_at(t) + HOPS

        @pl.when(t > 0)
        def _():
            for c in (1, 3):
                a = chan(c)
                arrived(fea.at[slot, a], gr.at[slot, a])

        pairs(slot, jnp.where(t == 0, 0, 2 * ATOMS))
        return carry

    lax.fori_loop(0, 2 * HOPS + 1, step, 0)

    kinds = jnp.broadcast_to(spe[HOPS], (C, ATOMS)) == 1
    centre = jnp.where(kinds, embb[3], embb[2])
    order_of = (0, 1, 1, 1, 2, 2, 2, 2, 2)
    sums = [None, None, None]
    weights = []
    for order in range(3):
        w = mix[order]
        high = w.astype(BF)
        low = (w - high.astype(F32)).astype(BF)
        weights.append((high, low))
    for m in range(NM):
        f = acc[:, m * ATOMS : (m + 1) * ATOMS] * centre
        high = f.astype(BF)
        low = (f - high.astype(F32)).astype(BF)
        w_high, w_low = weights[order_of[m]]
        mixed = (
            jnp.dot(w_high, high, preferred_element_type=F32)
            + jnp.dot(w_low, high, preferred_element_type=F32)
            + jnp.dot(w_high, low, preferred_element_type=F32)
        )
        square = mixed * mixed
        order = order_of[m]
        sums[order] = square if sums[order] is None else sums[order] + square
    for order in range(3):
        out_ref[order] = sums[order]

    for k in (1, 2, 3):
        for offset in (k, -k):
            for copy in sends(offset):
                copy.wait_send()
            for copy in relays(offset + HOPS):
                copy.wait_send()
    for copy in gathers:
        copy.wait_send()


def shards(
    positions,
    species,
    node_features,
    block_mask,
    radial_weight,
    species_embed,
    center_embed,
    mix_weight,
):
    n_blk = lax.axis_size("blk")
    box_x = float(n_blk) * slab_width
    dma = pltpu.SemaphoreType.DMA
    slots = 2 * HOPS + 1
    vmem = pltpu.VMEM
    sums = pl.pallas_call(
        functools.partial(kernel, box_x, n_blk),
        name="pair_descriptor",
        out_shape=jax.ShapeDtypeStruct((3, CD, ATOMS), F32),
        in_specs=[pl.BlockSpec(memory_space=pl.ANY)] * 8,
        out_specs=pl.BlockSpec(memory_space=pltpu.VMEM),
        scratch_shapes=[
            vmem((slots, 3, ATOMS), F32),
            vmem((slots, 1, ATOMS), jnp.int32),
            vmem((slots, CHANS, CD, ATOMS), F32),
            vmem((1, slots), jnp.int32),
            vmem((CHANS, NB, CD), F32),
            vmem((CHANS, 2, CD), F32),
            vmem((CHANS, 2, CD), F32),
            vmem((3, CD, C), F32),
            vmem((slots, 8, ATOMS), F32),
            vmem((NB, C, ATOMS), F32),
            vmem((4, C, ATOMS), F32),
            vmem((NB * ATOMS, NM * ATOMS), BF),
            vmem((C, NB * ATOMS), BF),
            vmem((C, NM * ATOMS), F32),
            dma((9,)),
            dma((slots, CHANS)),
            dma((slots, CHANS)),
            dma((slots,)),
            dma((slots,)),
            dma((slots,)),
            dma((slots,)),
            dma((slots, CHANS)),
            dma((slots, CHANS)),
            dma((3, CHANS)),
            dma((3, CHANS)),
        ],
        compiler_params=pltpu.CompilerParams(collective_id=0, has_side_effects=True),
    )(
        positions,
        species.reshape(1, ATOMS),
        node_features,
        block_mask,
        radial_weight,
        species_embed.T,
        center_embed.T,
        mix_weight,
    )
    return jnp.log1p(sums)


def solution(mesh):
    return jax.shard_map(
        shards,
        mesh=mesh,
        in_specs=(
            P(None, "blk"),
            P("blk"),
            P("chan", "blk"),
            P("blk", None),
            P(None, "chan"),
            P("chan", None),
            P("chan", None),
            P(),
        ),
        out_specs=P(None, "chan", "blk"),
        check_vma=False,
    )
```

time: 118 us -> 29.1 us (0.25)
  starting transfers between devices: 54.2 us -> 0 us
  Pallas kernels: 0 us -> 27.5 us
  waiting for transfers between devices: 22.9 us -> 0 us
  blocking collectives: 17.4 us -> 0 us
  other arithmetic: 10.6 us -> 0 us
  matrix products: 5.89 us -> 0 us
  between operations: 3.01 us -> 0.01 us
  loops' own time: 2.37 us -> 0 us
    ppermute x12 -> x0, starting transfers between devices: 54.2 us -> none  [from_behind(): lax.ppermute(value, axis, [(i, (i + by) % size) for i in range(size)])]
    pallas_call x0 -> x1, Pallas kernels: none -> 27.5 us  [shards(): pl.pallas_call(functools.partial(kernel, box_x, n_blk), name='pair_descri...]
    ppermute x12 -> x0, waiting for transfers between devices: 22.9 us -> none  [from_behind(): lax.ppermute(value, axis, [(i, (i + by) % size) for i in range(size)])]
    all_to_all x1 -> x0, blocking collectives: 17.4 us -> none  [sum_at_owner(): parts = lax.all_to_all(cut_along(value, dim, size), axis, 0, 0, tiled=True)]
    mul x9 -> x0, other arithmetic: 7.27 us -> none  [the longest x4 7.22 us: table_of(): math.sqrt(2.0 / cut_radius)]
    dot_general x13 -> x0, matrix products: 5.89 us -> none  [the longest x3 2.21 us: compute(): jnp.einsum('ncb,nmab->cma', other_carried, pair_table, preferred_element_...]
    another operation x3 -> x0, loops' own time: 2.37 us -> none  [contributions(): return lax.cond(active > 0, compute, skipped)]
    log1p x0 -> x1, local copies, waits for them, and re-layouts: none -> 1.36 us  [shards(): return jnp.log1p(sums)]
  transfers between devices with their start and end apart: 12 -> 0, of which waited for: 5 -> 0; matrix products, arithmetic and copies ran while one was open for 11% -> 0% of each run, Pallas kernels for 0% -> 0%
where the time goes in v1:
time: 29.1 us; the launch traced here: 28.9 us
  Pallas kernels  27.5 us (95%)
  local copies, waits for them, and re-layouts  1.36 us (5%)
    pallas_call x1, Pallas kernels, shards(): pl.pallas_call(functools.partial(kernel, box_x, n_blk), name='pair_descri...  27.5 us
    log1p x1, local copies, waits for them, and re-layouts, shards(): return jnp.log1p(sums)  1.36 us

profile of v1, /device:TPU:1, one launch (start us, length us, event | category | flops | bytes accessed | tf_op | source)
XLA Modules:
  0.0 28.9 jit_solution(9665745187347427964)
XLA Ops:
  0.0 27.5 %pair_descriptor.1 = f32[3,16,128]{2,1,0:T(8,128)} custom-call(f32[3,128]{1,0:T(4,128)} %pos_hbm.1, s32[1,128]{1,0:T(1,128)} %bitcast.5, f32[16,128]{1,0:T(8,128)} %fea_hbm.1, s32[1,7]{1,0:T(1,128)} %msk_hbm.1, f32[8,16]{1,0:T(8,128)} %rad_hbm.1, f32[2,16]{1,0:T(2,128)} %bitcast.3, f32[2,16]{1,0:T(2,128)} %bitcast.4, f32[3,64,64]{2,1,0:T(8,128)} %mix_hbm.1), custom_call_target="tpu_custom_call" | custom-call | tf_op jit(solution)/shard_map/pair_descriptor/pallas_call | solution.py:423
  27.5 1.4 %log1p.3 = f32[3,16,128]{2,1,0:T(8,128)} log-plus-one(f32[3,16,128]{2,1,0:T(8,128)} %pair_descriptor.1) | non-fusion elementwise | bytes 49152 | tf_op jit(solution)/shard_map/log1p | solution.py:467

commit v2 on v1

--- a/solution.py
+++ b/solution.py
@@ -47,6 +47,7 @@
 def kernel(
     box_x,
     n_blk,
+    row,
     pos_hbm,
     spe_hbm,
     fea_hbm,
@@ -67,7 +68,8 @@
     maskb,
     radb,
     embb,
-    tab,
+    tab_a,
+    tab_b,
     carr,
     acc,
     lsem,
@@ -77,7 +79,6 @@
     pr,
     ss,
     sr,
-    gs,
     gr,
     qs,
     qr,
@@ -86,6 +87,7 @@
     ch = lax.axis_index("chan")
     last = n_blk - HOPS
     late = me >= last
+    side = jnp.where(lax.rem(me, row) < row // 2, 1, -1)
     partner = ch + 1 - 2 * lax.rem(ch, 2)
 
     def slab(offset):
@@ -101,18 +103,6 @@
 
     def greet(offset, c):
         pl.semaphore_signal(barrier, inc=1, device_id=to(offset, c), device_id_type=MESH)
-
-    for c in (1, 2, 3):
-        greet(0, c)
-    for k in (1, 2, 3):
-        greet(-k, 0)
-        greet(-k, 2)
-    for k in (1, 2, 3):
-
-        @pl.when(me + k < last)
-        def _(k=k):
-            greet(k, 0)
-            greet(k, 2)
 
     first = [
         pltpu.make_async_copy(pos_hbm, pos.at[HOPS], lsem.at[0]),
@@ -130,12 +120,36 @@
             mix_hbm.at[:, pl.ds(pl.multiple_of(ch * CD, CD), CD), :], mix, lsem.at[7]
         ),
     ]
-    for copy in first + params + rest:
+    for copy in first:
+        copy.start()
+
+    ahead = jnp.logical_and(late, ch < 2)
+
+    def apart_in_z(c):
+        return chan(c) // 2 != ch // 2
+
+    for k in (3, 2, 1):
+        greet(-k, 0)
+        greet(-k, 2)
+    for c in (1, 2, 3):
+
+        @pl.when(jnp.logical_not(jnp.logical_and(late, jnp.logical_and(ch >= 2, apart_in_z(c)))))
+        def _(c=c):
+            greet(0, c)
+
+    for k in (1, 2, 3):
+
+        @pl.when(me + k < last + (k >= HOPS))
+        def _(k=k):
+            greet(k, 0)
+            greet(k, 2)
+
+    for copy in params + rest:
         copy.start()
     for copy in first:
         copy.wait()
-    lower = jnp.where(late, 0, jnp.minimum(me, HOPS))
-    pl.semaphore_wait(barrier, 3 + 2 * (HOPS + lower))
+    lower = jnp.where(late, jnp.where(me == last, 1, 0), jnp.minimum(me, HOPS))
+    pl.semaphore_wait(barrier, jnp.where(ahead, 1, 3) + 2 * (HOPS + lower))
 
     def sends(offset):
         slot = HOPS - offset
@@ -145,7 +159,7 @@
                 pltpu.make_async_remote_copy(
                     src_ref=fea.at[HOPS, ch],
                     dst_ref=fea.at[slot, ch],
-                    send_sem=fs.at[slot, c],
+                    send_sem=fs,
                     recv_sem=fr.at[slot, ch],
                     device_id=to(offset, c),
                     device_id_type=MESH,
@@ -155,7 +169,7 @@
             pltpu.make_async_remote_copy(
                 src_ref=pos.at[HOPS],
                 dst_ref=pos.at[slot],
-                send_sem=ps.at[slot],
+                send_sem=ps,
                 recv_sem=pr.at[slot],
                 device_id=to(offset, 0),
                 device_id_type=MESH,
@@ -165,7 +179,7 @@
             pltpu.make_async_remote_copy(
                 src_ref=spe.at[HOPS],
                 dst_ref=spe.at[slot],
-                send_sem=ss.at[slot],
+                send_sem=ss,
                 recv_sem=sr.at[slot],
                 device_id=to(offset, 0),
                 device_id_type=MESH,
@@ -173,29 +187,33 @@
         )
         return out
 
-    for k in (3, 2, 1):
-        for copy in sends(k):
+    nearest = jnp.where(late, n_blk - me, HOPS)
+    for turn in range(HOPS):
+        k = nearest + turn
+        for copy in sends(jnp.where(k > HOPS, k - HOPS, k)):
             copy.start()
+    def early(k):
+        return jnp.logical_and(me >= k, me < jnp.where(k >= HOPS, last + 1, last))
+
     for k in (1, 2, 3):
 
-        @pl.when(jnp.logical_and(me < last, me >= k))
+        @pl.when(early(k))
         def _(k=k):
             for copy in sends(-k):
                 copy.start()
 
     for copy in params:
         copy.wait()
-    gathers = []
-    for c in (1, 2, 3):
-        for q, (ref, sem, got) in enumerate(
-            (
-                (rad.at[ch], qs.at[0, c], qr.at[0, ch]),
-                (emb.at[ch], qs.at[1, c], qr.at[1, ch]),
-                (cen.at[ch], qs.at[2, c], qr.at[2, ch]),
-                (fea.at[HOPS, ch], gs.at[HOPS, c], gr.at[HOPS, ch]),
-            )
+
+    def gathers(c):
+        out = []
+        for ref, sem, got in (
+            (rad.at[ch], qs.at[0], qr.at[0, ch]),
+            (emb.at[ch], qs.at[1], qr.at[1, ch]),
+            (cen.at[ch], qs.at[2], qr.at[2, ch]),
+            (fea.at[HOPS, ch], fs, gr.at[HOPS, ch]),
         ):
-            gathers.append(
+            out.append(
                 pltpu.make_async_remote_copy(
                     src_ref=ref,
                     dst_ref=ref,
@@ -205,8 +223,14 @@
                     device_id_type=MESH,
                 )
             )
-    for copy in gathers:
-        copy.start()
+        return out
+
+    for c in (1, 2, 3):
+
+        @pl.when(jnp.logical_not(jnp.logical_and(ahead, apart_in_z(c))))
+        def _(c=c):
+            for copy in gathers(c):
+                copy.start()
 
     def relays(slot):
         out = []
@@ -216,7 +240,7 @@
                 pltpu.make_async_remote_copy(
                     src_ref=fea.at[slot, a],
                     dst_ref=fea.at[slot, a],
-                    send_sem=gs.at[slot, q],
+                    send_sem=fs,
                     recv_sem=gr.at[slot, a],
                     device_id={"blk": me, "chan": partner},
                     device_id_type=MESH,
@@ -245,6 +269,11 @@
         arrived(emb.at[a], qr.at[1, a])
         arrived(cen.at[a], qr.at[2, a])
         arrived(fea.at[HOPS, a], gr.at[HOPS, a])
+
+        @pl.when(jnp.logical_and(ahead, apart_in_z(c)))
+        def _(c=c):
+            for copy in gathers(c):
+                copy.start()
 
     eye = lax.broadcasted_iota(jnp.int32, (CD, CD), 0) == lax.broadcasted_iota(
         jnp.int32, (CD, CD), 1
@@ -271,8 +300,7 @@
 
     def offset_at(t):
         k = lax.rem(t + 2, 3) + 1
-        sign = jnp.where(late, -1, 1) * jnp.where(t <= 3, 1, -1)
-        return jnp.where(t == 0, 0, sign * k)
+        return jnp.where(t == 0, 0, jnp.where(t <= HOPS, side, -side) * k)
 
     def fetch(t):
         offset = offset_at(t)
@@ -285,19 +313,21 @@
         for copy in relays(slot):
             copy.start()
         k = lax.rem(t + 2, 3) + 1
-        early = jnp.logical_and(me < last, me >= k)
-
-        @pl.when(jnp.logical_and(offset < 0, jnp.logical_not(early)))
+
+        @pl.when(jnp.logical_and(offset < 0, jnp.logical_not(early(k))))
         def _():
             for copy in sends(offset):
                 copy.start()
 
-    def pairs(slot, apart):
+    def weigh(slot, tab):
         kinds = jnp.broadcast_to(spe[slot], (C, ATOMS)) == 1
         embedded = jnp.where(kinds, embb[1], embb[0])
         scaled = fea[slot].reshape(C, ATOMS) * embedded
         for n in range(NB):
             carr[:, n * ATOMS : (n + 1) * ATOMS] = (radb[n] * scaled).astype(BF)
+        acc[...] += jnp.dot(carr[...], tab[...], preferred_element_type=F32)
+
+    def table(slot, apart, tab):
         other = jnp.concatenate([pos[slot], jnp.zeros((5, ATOMS), F32)], axis=0)
         columns = jnp.transpose(other)
         keep = maskb[slot]
@@ -349,13 +379,8 @@
                 for m in range(NM):
                     value = radial[n] if m == 0 else radial[n] * harmonics[m]
                     tab[at, m * ATOMS : (m + 1) * ATOMS] = value.astype(BF)
-        acc[...] += jnp.dot(carr[...], tab[...], preferred_element_type=F32)
-
-    def step(t, carry):
-        @pl.when(t < 2 * HOPS)
-        def _():
-            fetch(t + 1)
-
+
+    def swapped(t):
         slot = offset_at(t) + HOPS
 
         @pl.when(t > 0)
@@ -364,10 +389,58 @@
                 a = chan(c)
                 arrived(fea.at[slot, a], gr.at[slot, a])
 
-        pairs(slot, jnp.where(t == 0, 0, 2 * ATOMS))
+        return slot
+
+    def advance(t, tab, other_tab):
+        fetch(t + 1)
+        slot = swapped(t)
+        weigh(slot, tab)
+        table(offset_at(t + 1) + HOPS, 2 * ATOMS, other_tab)
+
+    def finish(t, tab):
+        weigh(swapped(t), tab)
+
+    def side_of(i, carry):
+        t = i * (HOPS + 1)
+
+        @pl.when(i > 0)
+        def _():
+            fetch(t)
+
+        table(offset_at(t) + HOPS, jnp.where(i == 0, 0, 2 * ATOMS), tab_a)
+        advance(t, tab_a, tab_b)
+        advance(t + 1, tab_b, tab_a)
+
+        @pl.when(i == 0)
+        def _():
+            advance(t + 2, tab_a, tab_b)
+            finish(t + 3, tab_b)
+
+        @pl.when(i > 0)
+        def _():
+            finish(t + 2, tab_a)
+
         return carry
 
-    lax.fori_loop(0, 2 * HOPS + 1, step, 0)
+    lax.fori_loop(0, 2, side_of, 0)
+
+    def sent(ref, sem):
+        pltpu.make_async_remote_copy(
+            src_ref=ref,
+            dst_ref=ref,
+            send_sem=sem,
+            recv_sem=lsem.at[8],
+            device_id={"blk": me, "chan": partner},
+            device_id_type=MESH,
+        ).wait_send()
+
+    sent(fea.at[0 : 2 * HOPS], fs)
+    sent(fea.at[0, 0:3], fs)
+    sent(pos.at[0 : 2 * HOPS], ps)
+    sent(spe.at[0 : 2 * HOPS], ss)
+    sent(rad.at[0:3], qs.at[0])
+    sent(emb.at[0:3], qs.at[1])
+    sent(cen.at[0:3], qs.at[2])
 
     kinds = jnp.broadcast_to(spe[HOPS], (C, ATOMS)) == 1
     centre = jnp.where(kinds, embb[3], embb[2])
@@ -395,15 +468,6 @@
     for order in range(3):
         out_ref[order] = sums[order]
 
-    for k in (1, 2, 3):
-        for offset in (k, -k):
-            for copy in sends(offset):
-                copy.wait_send()
-            for copy in relays(offset + HOPS):
-                copy.wait_send()
-    for copy in gathers:
-        copy.wait_send()
-
 
 def shards(
     positions,
@@ -421,9 +485,9 @@
     slots = 2 * HOPS + 1
     vmem = pltpu.VMEM
     sums = pl.pallas_call(
-        functools.partial(kernel, box_x, n_blk),
+        functools.partial(kernel, box_x, n_blk, 8),
         name="pair_descriptor",
-        out_shape=jax.ShapeDtypeStruct((3, CD, ATOMS), F32),
+        out_shape=pltpu.VMEM((3, CD, ATOMS), F32),
         in_specs=[pl.BlockSpec(memory_space=pl.ANY)] * 8,
         out_specs=pl.BlockSpec(memory_space=pltpu.VMEM),
         scratch_shapes=[
@@ -439,18 +503,18 @@
             vmem((NB, C, ATOMS), F32),
             vmem((4, C, ATOMS), F32),
             vmem((NB * ATOMS, NM * ATOMS), BF),
+            vmem((NB * ATOMS, NM * ATOMS), BF),
             vmem((C, NB * ATOMS), BF),
             vmem((C, NM * ATOMS), F32),
             dma((9,)),
+            dma(()),
             dma((slots, CHANS)),
-            dma((slots, CHANS)),
+            dma(()),
             dma((slots,)),
-            dma((slots,)),
-            dma((slots,)),
+            dma(()),
             dma((slots,)),
             dma((slots, CHANS)),
-            dma((slots, CHANS)),
-            dma((3, CHANS)),
+            dma((3,)),
             dma((3, CHANS)),
         ],
         compiler_params=pltpu.CompilerParams(collective_id=0, has_side_effects=True),

time: 29.1 us -> 25.4 us (0.87)
  Pallas kernels: 27.5 us -> 24.5 us
  local copies, waits for them, and re-layouts: 1.36 us -> 0.62 us
    pallas_call x1, Pallas kernels: 27.5 us -> 24.5 us  [shards(): pl.pallas_call(functools.partial(kernel, box_x, n_blk, 8), name='pair_des...]
    log1p x1, local copies, waits for them, and re-layouts: 1.36 us -> 0.62 us  [shards(): return jnp.log1p(sums)]
where the time goes in v2:
time: 25.4 us; the launch traced here: 25.2 us
  Pallas kernels  24.5 us (96%)
  local copies, waits for them, and re-layouts  0.62 us (2%)
    pallas_call x1, Pallas kernels, shards(): pl.pallas_call(functools.partial(kernel, box_x, n_blk, 8), name='pair_des...  24.5 us
    log1p x1, local copies, waits for them, and re-layouts, shards(): return jnp.log1p(sums)  0.62 us

profile of v2, /device:TPU:1, one launch (start us, length us, event | category | flops | bytes accessed | tf_op | source)
XLA Modules:
  0.0 25.2 jit_solution(5035201932442247117)
XLA Ops:
  0.0 24.5 %pair_descriptor.1 = f32[3,16,128]{2,1,0:T(8,128)S(1)} custom-call(f32[3,128]{1,0:T(4,128)} %pos_hbm.1, s32[1,128]{1,0:T(1,128)} %bitcast.5, f32[16,128]{1,0:T(8,128)} %fea_hbm.1, s32[1,7]{1,0:T(1,128)} %msk_hbm.1, f32[8,16]{1,0:T(8,128)} %rad_hbm.1, f32[2,16]{1,0:T(2,128)} %bitcast.3, f32[2,16]{1,0:T(2,128)} %bitcast.4, f32[3,64,64]{2,1,0:T(8,128)} %mix_hbm.1), custom_call_target="tpu_custom_call" | custom-call | tf_op jit(solution)/shard_map/pair_descriptor/pallas_call | solution.py:487
  24.6 0.6 %log1p.3 = f32[3,16,128]{2,1,0:T(8,128)} log-plus-one(f32[3,16,128]{2,1,0:T(8,128)S(1)} %pair_descriptor.1) | non-fusion elementwise | bytes 49152 | tf_op jit(solution)/shard_map/log1p | solution.py:531

commit v3 on v2

--- a/solution.py
+++ b/solution.py
@@ -23,6 +23,7 @@
 NB = 8
 NM = 9
 HALF = 16
+PIECES = 5
 BF = jnp.bfloat16
 F32 = jnp.float32
 
@@ -61,9 +62,7 @@
     spe,
     fea,
     msk,
-    rad,
-    emb,
-    cen,
+    prm,
     mix,
     maskb,
     radb,
@@ -79,7 +78,6 @@
     pr,
     ss,
     sr,
-    gr,
     qs,
     qr,
 ):
@@ -110,9 +108,9 @@
         pltpu.make_async_copy(fea_hbm, fea.at[HOPS, ch], lsem.at[2]),
     ]
     params = [
-        pltpu.make_async_copy(rad_hbm, rad.at[ch], lsem.at[3]),
-        pltpu.make_async_copy(sem_hbm, emb.at[ch], lsem.at[4]),
-        pltpu.make_async_copy(cem_hbm, cen.at[ch], lsem.at[5]),
+        pltpu.make_async_copy(rad_hbm, prm.at[ch, 0], lsem.at[3]),
+        pltpu.make_async_copy(sem_hbm, prm.at[ch, 1, 0:2], lsem.at[4]),
+        pltpu.make_async_copy(cem_hbm, prm.at[ch, 2, 0:2], lsem.at[5]),
     ]
     rest = [
         pltpu.make_async_copy(msk_hbm, msk, lsem.at[6]),
@@ -123,6 +121,9 @@
     for copy in first:
         copy.start()
 
+    directs = jnp.logical_and(late, lax.rem(ch, 2) == 0)
+    spared = jnp.logical_and(me == 0, ch == 0)
+
     ahead = jnp.logical_and(late, ch < 2)
 
     def apart_in_z(c):
@@ -131,6 +132,13 @@
     for k in (3, 2, 1):
         greet(-k, 0)
         greet(-k, 2)
+
+    @pl.when(jnp.logical_and(me == 0, ch == 1))
+    def _():
+        for k in (3, 2, 1):
+            greet(-k, 1)
+            greet(-k, 3)
+
     for c in (1, 2, 3):
 
         @pl.when(jnp.logical_not(jnp.logical_and(late, jnp.logical_and(ch >= 2, apart_in_z(c)))))
@@ -149,7 +157,7 @@
     for copy in first:
         copy.wait()
     lower = jnp.where(late, jnp.where(me == last, 1, 0), jnp.minimum(me, HOPS))
-    pl.semaphore_wait(barrier, jnp.where(ahead, 1, 3) + 2 * (HOPS + lower))
+    pl.semaphore_wait(barrier, jnp.where(ahead, 1, 3) + 2 * (HOPS + lower) + directs.astype(jnp.int32))
 
     def sends(offset):
         slot = HOPS - offset
@@ -160,7 +168,7 @@
                     src_ref=fea.at[HOPS, ch],
                     dst_ref=fea.at[slot, ch],
                     send_sem=fs,
-                    recv_sem=fr.at[slot, ch],
+                    recv_sem=fr.at[slot, 0],
                     device_id=to(offset, c),
                     device_id_type=MESH,
                 )
@@ -188,6 +196,21 @@
         return out
 
     nearest = jnp.where(late, n_blk - me, HOPS)
+
+    def direct():
+        return pltpu.make_async_remote_copy(
+            src_ref=fea.at[HOPS, ch],
+            dst_ref=fea.at[HOPS - nearest, ch],
+            send_sem=fs,
+            recv_sem=fr.at[HOPS - nearest, 1],
+            device_id={"blk": 0, "chan": 1},
+            device_id_type=MESH,
+        )
+
+    @pl.when(directs)
+    def _():
+        direct().start()
+
     for turn in range(HOPS):
         k = nearest + turn
         for copy in sends(jnp.where(k > HOPS, k - HOPS, k)):
@@ -208,10 +231,8 @@
     def gathers(c):
         out = []
         for ref, sem, got in (
-            (rad.at[ch], qs.at[0], qr.at[0, ch]),
-            (emb.at[ch], qs.at[1], qr.at[1, ch]),
-            (cen.at[ch], qs.at[2], qr.at[2, ch]),
-            (fea.at[HOPS, ch], fs, gr.at[HOPS, ch]),
+            (prm.at[ch], qs, qr),
+            (fea.at[HOPS, ch], fs, fr.at[HOPS, 0]),
         ):
             out.append(
                 pltpu.make_async_remote_copy(
@@ -241,7 +262,7 @@
                     src_ref=fea.at[slot, a],
                     dst_ref=fea.at[slot, a],
                     send_sem=fs,
-                    recv_sem=gr.at[slot, a],
+                    recv_sem=fr.at[slot, 1],
                     device_id={"blk": me, "chan": partner},
                     device_id_type=MESH,
                 )
@@ -263,12 +284,9 @@
     for s in range(2 * HOPS + 1):
         maskb[s] = jnp.broadcast_to(msk[:, s : s + 1].astype(F32), (8, ATOMS))
 
+    arrived(prm.at[0:3], qr)
+    arrived(fea.at[0, 0:3], fr.at[HOPS, 0])
     for c in (1, 2, 3):
-        a = chan(c)
-        arrived(rad.at[a], qr.at[0, a])
-        arrived(emb.at[a], qr.at[1, a])
-        arrived(cen.at[a], qr.at[2, a])
-        arrived(fea.at[HOPS, a], gr.at[HOPS, a])
 
         @pl.when(jnp.logical_and(ahead, apart_in_z(c)))
         def _(c=c):
@@ -281,12 +299,12 @@
     for q in range(CHANS):
         rows = slice(q * CD, (q + 1) * CD)
         for n in range(NB):
-            row = jnp.broadcast_to(rad[q, n : n + 1, :], (CD, CD))
+            row = jnp.broadcast_to(prm[q, 0, n : n + 1, :], (CD, CD))
             column = jnp.sum(jnp.where(eye, row, 0.0), axis=1, keepdims=True)
             radb[n, rows, :] = jnp.broadcast_to(column, (CD, ATOMS))
         for kind in (0, 1):
-            for at, ref in ((kind, emb), (2 + kind, cen)):
-                row = jnp.broadcast_to(ref[q, kind : kind + 1, :], (CD, CD))
+            for at, of in ((kind, 1), (2 + kind, 2)):
+                row = jnp.broadcast_to(prm[q, of, kind : kind + 1, :], (CD, CD))
                 column = jnp.sum(jnp.where(eye, row, 0.0), axis=1, keepdims=True)
                 embb[at, rows, :] = jnp.broadcast_to(column, (CD, ATOMS))
 
@@ -298,8 +316,11 @@
     root3 = math.sqrt(3.0)
     ratio = math.sqrt(5.0 / 3.0)
 
+    def reach_at(t):
+        return jnp.where(jnp.logical_and(late, t <= HOPS), HOPS + 1 - t, lax.rem(t + 2, 3) + 1)
+
     def offset_at(t):
-        k = lax.rem(t + 2, 3) + 1
+        k = reach_at(t)
         return jnp.where(t == 0, 0, jnp.where(t <= HOPS, side, -side) * k)
 
     def fetch(t):
@@ -307,32 +328,39 @@
         slot = offset + HOPS
         arrived(pos.at[slot], pr.at[slot])
         arrived(spe.at[slot], sr.at[slot])
-        for c in (0, 2):
-            a = chan(c)
-            arrived(fea.at[slot, a], fr.at[slot, a])
-        for copy in relays(slot):
-            copy.start()
-        k = lax.rem(t + 2, 3) + 1
+        arrived(fea.at[0, 0:2], fr.at[slot, 0])
+
+        @pl.when(jnp.logical_not(jnp.logical_and(spared, offset < 0)))
+        def _():
+            for copy in relays(slot):
+                copy.start()
+
+        k = reach_at(t)
 
         @pl.when(jnp.logical_and(offset < 0, jnp.logical_not(early(k))))
         def _():
             for copy in sends(offset):
                 copy.start()
 
-    def weigh(slot, tab):
+    def weigh(slot):
         kinds = jnp.broadcast_to(spe[slot], (C, ATOMS)) == 1
         embedded = jnp.where(kinds, embb[1], embb[0])
         scaled = fea[slot].reshape(C, ATOMS) * embedded
         for n in range(NB):
             carr[:, n * ATOMS : (n + 1) * ATOMS] = (radb[n] * scaled).astype(BF)
-        acc[...] += jnp.dot(carr[...], tab[...], preferred_element_type=F32)
-
-    def table(slot, apart, tab):
+
+    def product(tab, piece):
+        at = slice(piece * 2 * ATOMS, min((piece + 1) * 2, NM) * ATOMS)
+        acc[:, at] += jnp.dot(carr[...], tab[:, at], preferred_element_type=F32)
+
+    def table(slot, apart, tab, between=None):
         other = jnp.concatenate([pos[slot], jnp.zeros((5, ATOMS), F32)], axis=0)
         columns = jnp.transpose(other)
         keep = maskb[slot]
         keep = jnp.concatenate([keep, keep], axis=0)
         for tile in range(ATOMS // HALF):
+            if between is not None and tile < PIECES:
+                product(between, tile)
             rows = slice(tile * HALF, (tile + 1) * HALF)
             dx = columns[rows, 0:1] - own_x
             dy = columns[rows, 1:2] - own_y
@@ -385,20 +413,20 @@
 
         @pl.when(t > 0)
         def _():
-            for c in (1, 3):
-                a = chan(c)
-                arrived(fea.at[slot, a], gr.at[slot, a])
+            arrived(fea.at[0, 0:2], fr.at[slot, 1])
 
         return slot
 
     def advance(t, tab, other_tab):
         fetch(t + 1)
         slot = swapped(t)
-        weigh(slot, tab)
-        table(offset_at(t + 1) + HOPS, 2 * ATOMS, other_tab)
+        weigh(slot)
+        table(offset_at(t + 1) + HOPS, 2 * ATOMS, other_tab, tab)
 
     def finish(t, tab):
-        weigh(swapped(t), tab)
+        weigh(swapped(t))
+        for piece in range(PIECES):
+            product(tab, piece)
 
     def side_of(i, carry):
         t = i * (HOPS + 1)
@@ -434,13 +462,21 @@
             device_id_type=MESH,
         ).wait_send()
 
-    sent(fea.at[0 : 2 * HOPS], fs)
-    sent(fea.at[0, 0:3], fs)
+    sent(fea.at[0:5], fs)
+    sent(fea.at[0, 0], fs)
+
+    @pl.when(jnp.logical_not(spared))
+    def _():
+        sent(fea.at[0:1], fs)
+        sent(fea.at[0, 0:2], fs)
+
+    @pl.when(directs)
+    def _():
+        sent(fea.at[0, 0], fs)
+
     sent(pos.at[0 : 2 * HOPS], ps)
     sent(spe.at[0 : 2 * HOPS], ss)
-    sent(rad.at[0:3], qs.at[0])
-    sent(emb.at[0:3], qs.at[1])
-    sent(cen.at[0:3], qs.at[2])
+    sent(prm.at[0:3], qs)
 
     kinds = jnp.broadcast_to(spe[HOPS], (C, ATOMS)) == 1
     centre = jnp.where(kinds, embb[3], embb[2])
@@ -495,9 +531,7 @@
             vmem((slots, 1, ATOMS), jnp.int32),
             vmem((slots, CHANS, CD, ATOMS), F32),
             vmem((1, slots), jnp.int32),
-            vmem((CHANS, NB, CD), F32),
-            vmem((CHANS, 2, CD), F32),
-            vmem((CHANS, 2, CD), F32),
+            vmem((CHANS, 3, NB, CD), F32),
             vmem((3, CD, C), F32),
             vmem((slots, 8, ATOMS), F32),
             vmem((NB, C, ATOMS), F32),
@@ -508,14 +542,13 @@
             vmem((C, NM * ATOMS), F32),
             dma((9,)),
             dma(()),
-            dma((slots, CHANS)),
+            dma((slots, 2)),
             dma(()),
             dma((slots,)),
             dma(()),
             dma((slots,)),
-            dma((slots, CHANS)),
-            dma((3,)),
-            dma((3, CHANS)),
+            dma(()),
+            dma(()),
         ],
         compiler_params=pltpu.CompilerParams(collective_id=0, has_side_effects=True),
     )(

time: 25.4 us -> 23.4 us (0.921)
  Pallas kernels: 24.5 us -> 22.6 us
    pallas_call x1, Pallas kernels: 24.5 us -> 22.6 us  [shards(): pl.pallas_call(functools.partial(kernel, box_x, n_blk, 8), name='pair_des...]
where the time goes in v3:
time: 23.4 us; the launch traced here: 23.2 us
  Pallas kernels  22.6 us (97%)
  local copies, waits for them, and re-layouts  0.62 us (3%)
    pallas_call x1, Pallas kernels, shards(): pl.pallas_call(functools.partial(kernel, box_x, n_blk, 8), name='pair_des...  22.6 us
    log1p x1, local copies, waits for them, and re-layouts, shards(): return jnp.log1p(sums)  0.62 us

profile of v3, /device:TPU:1, one launch (start us, length us, event | category | flops | bytes accessed | tf_op | source)
XLA Modules:
  0.0 23.2 jit_solution(11853031174092023331)
XLA Ops:
  0.0 22.6 %pair_descriptor.1 = f32[3,16,128]{2,1,0:T(8,128)S(1)} custom-call(f32[3,128]{1,0:T(4,128)} %pos_hbm.1, s32[1,128]{1,0:T(1,128)} %bitcast.5, f32[16,128]{1,0:T(8,128)} %fea_hbm.1, s32[1,7]{1,0:T(1,128)} %msk_hbm.1, f32[8,16]{1,0:T(8,128)} %rad_hbm.1, f32[2,16]{1,0:T(2,128)} %bitcast.3, f32[2,16]{1,0:T(2,128)} %bitcast.4, f32[3,64,64]{2,1,0:T(8,128)} %mix_hbm.1), custom_call_target="tpu_custom_call" | custom-call | tf_op jit(solution)/shard_map/pair_descriptor/pallas_call | solution.py:523
  22.6 0.6 %log1p.3 = f32[3,16,128]{2,1,0:T(8,128)} log-plus-one(f32[3,16,128]{2,1,0:T(8,128)S(1)} %pair_descriptor.1) | non-fusion elementwise | bytes 49152 | tf_op jit(solution)/shard_map/log1p | solution.py:564

commit v4 on v3

--- a/solution.py
+++ b/solution.py
@@ -64,6 +64,7 @@
     msk,
     prm,
     mix,
+    split,
     maskb,
     radb,
     embb,
@@ -85,7 +86,7 @@
     ch = lax.axis_index("chan")
     last = n_blk - HOPS
     late = me >= last
-    side = jnp.where(lax.rem(me, row) < row // 2, 1, -1)
+    side = jnp.where(jnp.logical_and(lax.rem(me, row) < row // 2, me < last - HOPS), 1, -1)
     partner = ch + 1 - 2 * lax.rem(ch, 2)
 
     def slab(offset):
@@ -121,8 +122,9 @@
     for copy in first:
         copy.start()
 
-    directs = jnp.logical_and(late, lax.rem(ch, 2) == 0)
-    spared = jnp.logical_and(me == 0, ch == 0)
+    even_late = jnp.logical_and(late, lax.rem(ch, 2) == 0)
+    served = jnp.logical_and(me == 0, ch == 0)
+    lone = jnp.logical_and(me == 0, ch == 1)
 
     ahead = jnp.logical_and(late, ch < 2)
 
@@ -133,7 +135,7 @@
         greet(-k, 0)
         greet(-k, 2)
 
-    @pl.when(jnp.logical_and(me == 0, ch == 1))
+    @pl.when(lone)
     def _():
         for k in (3, 2, 1):
             greet(-k, 1)
@@ -157,12 +159,25 @@
     for copy in first:
         copy.wait()
     lower = jnp.where(late, jnp.where(me == last, 1, 0), jnp.minimum(me, HOPS))
-    pl.semaphore_wait(barrier, jnp.where(ahead, 1, 3) + 2 * (HOPS + lower) + directs.astype(jnp.int32))
+    straights = even_late.astype(jnp.int32)
+    pl.semaphore_wait(barrier, jnp.where(ahead, 1, 3) + 2 * (HOPS + lower) + straights)
 
     def sends(offset):
         slot = HOPS - offset
         out = []
-        for c in (0, 2):
+        for ref, sem, got in ((pos, ps, pr), (spe, ss, sr)):
+            out.append(
+                pltpu.make_async_remote_copy(
+                    src_ref=ref.at[HOPS],
+                    dst_ref=ref.at[slot],
+                    send_sem=sem,
+                    recv_sem=got.at[slot],
+                    device_id=to(offset, 0),
+                    device_id_type=MESH,
+                )
+            )
+        lower_chip = jnp.where(ch >= 2, 2, 0)
+        for c in (lower_chip, 2 - lower_chip):
             out.append(
                 pltpu.make_async_remote_copy(
                     src_ref=fea.at[HOPS, ch],
@@ -173,48 +188,30 @@
                     device_id_type=MESH,
                 )
             )
-        out.append(
-            pltpu.make_async_remote_copy(
-                src_ref=pos.at[HOPS],
-                dst_ref=pos.at[slot],
-                send_sem=ps,
-                recv_sem=pr.at[slot],
-                device_id=to(offset, 0),
-                device_id_type=MESH,
-            )
-        )
-        out.append(
-            pltpu.make_async_remote_copy(
-                src_ref=spe.at[HOPS],
-                dst_ref=spe.at[slot],
-                send_sem=ss,
-                recv_sem=sr.at[slot],
-                device_id=to(offset, 0),
-                device_id_type=MESH,
-            )
-        )
         return out
 
     nearest = jnp.where(late, n_blk - me, HOPS)
 
-    def direct():
+    def direct(target):
+        slot = HOPS - nearest
         return pltpu.make_async_remote_copy(
             src_ref=fea.at[HOPS, ch],
-            dst_ref=fea.at[HOPS - nearest, ch],
+            dst_ref=fea.at[slot, ch],
             send_sem=fs,
-            recv_sem=fr.at[HOPS - nearest, 1],
-            device_id={"blk": 0, "chan": 1},
+            recv_sem=fr.at[slot, 1],
+            device_id={"blk": 0, "chan": target},
             device_id_type=MESH,
         )
 
-    @pl.when(directs)
+    @pl.when(even_late)
     def _():
-        direct().start()
+        direct(1).start()
 
     for turn in range(HOPS):
         k = nearest + turn
         for copy in sends(jnp.where(k > HOPS, k - HOPS, k)):
             copy.start()
+
     def early(k):
         return jnp.logical_and(me >= k, me < jnp.where(k >= HOPS, last + 1, last))
 
@@ -281,6 +278,12 @@
 
     for copy in rest:
         copy.wait()
+    for order in range(3):
+        w = mix[order]
+        high = w.astype(BF)
+        split[order, :, 0:C] = high
+        split[order, :, C : 2 * C] = (w - high.astype(F32)).astype(BF)
+        split[order, :, 2 * C : 3 * C] = high
     for s in range(2 * HOPS + 1):
         maskb[s] = jnp.broadcast_to(msk[:, s : s + 1].astype(F32), (8, ATOMS))
 
@@ -323,14 +326,21 @@
         k = reach_at(t)
         return jnp.where(t == 0, 0, jnp.where(t <= HOPS, side, -side) * k)
 
+    def placed(t):
+        slot = offset_at(t) + HOPS
+        arrived(pos.at[slot], pr.at[slot])
+
     def fetch(t):
+        placed(t)
+        fill(t)
+
+    def fill(t):
         offset = offset_at(t)
         slot = offset + HOPS
-        arrived(pos.at[slot], pr.at[slot])
         arrived(spe.at[slot], sr.at[slot])
         arrived(fea.at[0, 0:2], fr.at[slot, 0])
 
-        @pl.when(jnp.logical_not(jnp.logical_and(spared, offset < 0)))
+        @pl.when(jnp.logical_not(jnp.logical_and(served, offset < 0)))
         def _():
             for copy in relays(slot):
                 copy.start()
@@ -437,7 +447,18 @@
 
         table(offset_at(t) + HOPS, jnp.where(i == 0, 0, 2 * ATOMS), tab_a)
         advance(t, tab_a, tab_b)
-        advance(t + 1, tab_b, tab_a)
+        alone = jnp.logical_and(lone, i > 0)
+
+        @pl.when(jnp.logical_not(alone))
+        def _():
+            advance(t + 1, tab_b, tab_a)
+
+        @pl.when(alone)
+        def _():
+            finish(t + 1, tab_b)
+            placed(t + 2)
+            table(offset_at(t + 2) + HOPS, 2 * ATOMS, tab_a)
+            fill(t + 2)
 
         @pl.when(i == 0)
         def _():
@@ -451,6 +472,22 @@
         return carry
 
     lax.fori_loop(0, 2, side_of, 0)
+
+    kinds = jnp.broadcast_to(spe[HOPS], (C, ATOMS)) == 1
+    centre = jnp.where(kinds, embb[3], embb[2])
+    for order, (start, stop) in enumerate(((0, 1), (1, 4), (4, 9))):
+        at = slice(start * ATOMS, stop * ATOMS)
+        f = acc[:, at] * jnp.concatenate([centre] * (stop - start), axis=1)
+        high = f.astype(BF)
+        low = (f - high.astype(F32)).astype(BF)
+        mixed = jnp.dot(
+            split[order], jnp.concatenate([high, high, low], axis=0), preferred_element_type=F32
+        )
+        square = mixed * mixed
+        total = square[:, 0:ATOMS]
+        for m in range(1, stop - start):
+            total = total + square[:, m * ATOMS : (m + 1) * ATOMS]
+        out_ref[order] = total
 
     def sent(ref, sem):
         pltpu.make_async_remote_copy(
@@ -464,45 +501,18 @@
 
     sent(fea.at[0:5], fs)
     sent(fea.at[0, 0], fs)
-
-    @pl.when(jnp.logical_not(spared))
-    def _():
-        sent(fea.at[0:1], fs)
-        sent(fea.at[0, 0:2], fs)
-
-    @pl.when(directs)
-    def _():
-        sent(fea.at[0, 0], fs)
-
     sent(pos.at[0 : 2 * HOPS], ps)
     sent(spe.at[0 : 2 * HOPS], ss)
     sent(prm.at[0:3], qs)
 
-    kinds = jnp.broadcast_to(spe[HOPS], (C, ATOMS)) == 1
-    centre = jnp.where(kinds, embb[3], embb[2])
-    order_of = (0, 1, 1, 1, 2, 2, 2, 2, 2)
-    sums = [None, None, None]
-    weights = []
-    for order in range(3):
-        w = mix[order]
-        high = w.astype(BF)
-        low = (w - high.astype(F32)).astype(BF)
-        weights.append((high, low))
-    for m in range(NM):
-        f = acc[:, m * ATOMS : (m + 1) * ATOMS] * centre
-        high = f.astype(BF)
-        low = (f - high.astype(F32)).astype(BF)
-        w_high, w_low = weights[order_of[m]]
-        mixed = (
-            jnp.dot(w_high, high, preferred_element_type=F32)
-            + jnp.dot(w_low, high, preferred_element_type=F32)
-            + jnp.dot(w_high, low, preferred_element_type=F32)
-        )
-        square = mixed * mixed
-        order = order_of[m]
-        sums[order] = square if sums[order] is None else sums[order] + square
-    for order in range(3):
-        out_ref[order] = sums[order]
+    @pl.when(jnp.logical_not(served))
+    def _():
+        sent(fea.at[0], fs)
+        sent(fea.at[0, 0:2], fs)
+
+    @pl.when(even_late)
+    def _():
+        sent(fea.at[0, 0], fs)
 
 
 def shards(
@@ -533,6 +543,7 @@
             vmem((1, slots), jnp.int32),
             vmem((CHANS, 3, NB, CD), F32),
             vmem((3, CD, C), F32),
+            vmem((3, CD, 3 * C), BF),
             vmem((slots, 8, ATOMS), F32),
             vmem((NB, C, ATOMS), F32),
             vmem((4, C, ATOMS), F32),

time: 23.4 us -> 23.2 us (level)
  no operation moved by 1% of the time
where the time goes in v4:
time: 23.2 us; the launch traced here: 23 us
  Pallas kernels  22.4 us (97%)
  local copies, waits for them, and re-layouts  0.62 us (3%)
    pallas_call x1, Pallas kernels, shards(): pl.pallas_call(functools.partial(kernel, box_x, n_blk, 8), name='pair_des...  22.4 us
    log1p x1, local copies, waits for them, and re-layouts, shards(): return jnp.log1p(sums)  0.62 us

profile of v4, /device:TPU:1, one launch (start us, length us, event | category | flops | bytes accessed | tf_op | source)
XLA Modules:
  0.0 23.0 jit_solution(15487696386709028063)
XLA Ops:
  0.0 22.4 %pair_descriptor.1 = f32[3,16,128]{2,1,0:T(8,128)S(1)} custom-call(f32[3,128]{1,0:T(4,128)} %pos_hbm.1, s32[1,128]{1,0:T(1,128)} %bitcast.5, f32[16,128]{1,0:T(8,128)} %fea_hbm.1, s32[1,7]{1,0:T(1,128)} %msk_hbm.1, f32[8,16]{1,0:T(8,128)} %rad_hbm.1, f32[2,16]{1,0:T(2,128)} %bitcast.3, f32[2,16]{1,0:T(2,128)} %bitcast.4, f32[3,64,64]{2,1,0:T(8,128)} %mix_hbm.1), custom_call_target="tpu_custom_call" | custom-call | tf_op jit(solution)/shard_map/pair_descriptor/pallas_call | solution.py:533
  22.4 0.6 %log1p.3 = f32[3,16,128]{2,1,0:T(8,128)} log-plus-one(f32[3,16,128]{2,1,0:T(8,128)S(1)} %pair_descriptor.1) | non-fusion elementwise | bytes 49152 | tf_op jit(solution)/shard_map/log1p | solution.py:575

commit v5 on v4

--- a/solution.py
+++ b/solution.py
@@ -131,9 +131,15 @@
     def apart_in_z(c):
         return chan(c) // 2 != ch // 2
 
+    def crossing(offset):
+        return jnp.logical_and(late, jnp.logical_and(me + offset >= last, me + offset < n_blk))
+
     for k in (3, 2, 1):
         greet(-k, 0)
-        greet(-k, 2)
+
+        @pl.when(jnp.logical_not(crossing(-k)))
+        def _(k=k):
+            greet(-k, 2)
 
     @pl.when(lone)
     def _():
@@ -149,7 +155,7 @@
 
     for k in (1, 2, 3):
 
-        @pl.when(me + k < last + (k >= HOPS))
+        @pl.when(me + k < last)
         def _(k=k):
             greet(k, 0)
             greet(k, 2)
@@ -158,9 +164,9 @@
         copy.start()
     for copy in first:
         copy.wait()
-    lower = jnp.where(late, jnp.where(me == last, 1, 0), jnp.minimum(me, HOPS))
+    lower = jnp.where(late, 0, jnp.minimum(me, HOPS))
     straights = even_late.astype(jnp.int32)
-    pl.semaphore_wait(barrier, jnp.where(ahead, 1, 3) + 2 * (HOPS + lower) + straights)
+    pl.semaphore_wait(barrier, jnp.where(ahead, 1, 3) + 2 * (HOPS + lower) + straights - jnp.where(late, n_blk - 1 - me, 0))
 
     def sends(offset):
         slot = HOPS - offset
@@ -176,8 +182,7 @@
                     device_id_type=MESH,
                 )
             )
-        lower_chip = jnp.where(ch >= 2, 2, 0)
-        for c in (lower_chip, 2 - lower_chip):
+        for c in (0, 2):
             out.append(
                 pltpu.make_async_remote_copy(
                     src_ref=fea.at[HOPS, ch],
@@ -190,6 +195,15 @@
             )
         return out
 
+    def begin(offset):
+        copies = sends(offset)
+        for copy in copies[:3]:
+            copy.start()
+
+        @pl.when(jnp.logical_not(crossing(offset)))
+        def _():
+            copies[3].start()
+
     nearest = jnp.where(late, n_blk - me, HOPS)
 
     def direct(target):
@@ -209,18 +223,16 @@
 
     for turn in range(HOPS):
         k = nearest + turn
-        for copy in sends(jnp.where(k > HOPS, k - HOPS, k)):
-            copy.start()
+        begin(jnp.where(k > HOPS, k - HOPS, k))
 
     def early(k):
-        return jnp.logical_and(me >= k, me < jnp.where(k >= HOPS, last + 1, last))
+        return jnp.logical_and(me >= k, me < last)
 
     for k in (1, 2, 3):
 
         @pl.when(early(k))
         def _(k=k):
-            for copy in sends(-k):
-                copy.start()
+            begin(-k)
 
     for copy in params:
         copy.wait()
@@ -320,7 +332,7 @@
     ratio = math.sqrt(5.0 / 3.0)
 
     def reach_at(t):
-        return jnp.where(jnp.logical_and(late, t <= HOPS), HOPS + 1 - t, lax.rem(t + 2, 3) + 1)
+        return lax.rem(t + 2, 3) + 1
 
     def offset_at(t):
         k = reach_at(t)
@@ -338,19 +350,42 @@
         offset = offset_at(t)
         slot = offset + HOPS
         arrived(spe.at[slot], sr.at[slot])
-        arrived(fea.at[0, 0:2], fr.at[slot, 0])
+        swap = crossing(offset)
+        k = reach_at(t)
+        answers = jnp.logical_and(offset < 0, jnp.logical_not(early(k)))
+
+        @pl.when(swap)
+        def _():
+            arrived(fea.at[0, 0], fr.at[slot, 0])
+
+            @pl.when(answers)
+            def _():
+                begin(offset)
+
+            pltpu.make_async_remote_copy(
+                src_ref=fea.at[slot, ch],
+                dst_ref=fea.at[slot, ch],
+                send_sem=fs,
+                recv_sem=fr.at[slot, 2],
+                device_id=to(0, 2),
+                device_id_type=MESH,
+            ).start()
+            arrived(fea.at[0, 0], fr.at[slot, 2])
+
+        @pl.when(jnp.logical_not(swap))
+        def _():
+            arrived(fea.at[0, 0:2], fr.at[slot, 0])
+
+            @pl.when(answers)
+            def _():
+                begin(offset)
+
 
         @pl.when(jnp.logical_not(jnp.logical_and(served, offset < 0)))
         def _():
             for copy in relays(slot):
                 copy.start()
 
-        k = reach_at(t)
-
-        @pl.when(jnp.logical_and(offset < 0, jnp.logical_not(early(k))))
-        def _():
-            for copy in sends(offset):
-                copy.start()
 
     def weigh(slot):
         kinds = jnp.broadcast_to(spe[slot], (C, ATOMS)) == 1
@@ -553,7 +588,7 @@
             vmem((C, NM * ATOMS), F32),
             dma((9,)),
             dma(()),
-            dma((slots, 2)),
+            dma((slots, 3)),
             dma(()),
             dma((slots,)),
             dma(()),

time: 23.2 us -> 23.1 us (level)
  no operation moved by 1% of the time
where the time goes in v5:
time: 23.1 us; the launch traced here: 22.9 us
  Pallas kernels  22.2 us (96%)
  local copies, waits for them, and re-layouts  0.62 us (3%)
    pallas_call x1, Pallas kernels, shards(): pl.pallas_call(functools.partial(kernel, box_x, n_blk, 8), name='pair_des...  22.2 us
    log1p x1, local copies, waits for them, and re-layouts, shards(): return jnp.log1p(sums)  0.62 us

profile of v5, /device:TPU:1, one launch (start us, length us, event | category | flops | bytes accessed | tf_op | source)
XLA Modules:
  0.0 22.9 jit_solution(1042421250147753417)
XLA Ops:
  0.0 22.2 %pair_descriptor.1 = f32[3,16,128]{2,1,0:T(8,128)S(1)} custom-call(f32[3,128]{1,0:T(4,128)} %pos_hbm.1, s32[1,128]{1,0:T(1,128)} %bitcast.5, f32[16,128]{1,0:T(8,128)} %fea_hbm.1, s32[1,7]{1,0:T(1,128)} %msk_hbm.1, f32[8,16]{1,0:T(8,128)} %rad_hbm.1, f32[2,16]{1,0:T(2,128)} %bitcast.3, f32[2,16]{1,0:T(2,128)} %bitcast.4, f32[3,64,64]{2,1,0:T(8,128)} %mix_hbm.1), custom_call_target="tpu_custom_call" | custom-call | tf_op jit(solution)/shard_map/pair_descriptor/pallas_call | solution.py:568
  22.3 0.6 %log1p.3 = f32[3,16,128]{2,1,0:T(8,128)} log-plus-one(f32[3,16,128]{2,1,0:T(8,128)S(1)} %pair_descriptor.1) | non-fusion elementwise | bytes 49152 | tf_op jit(solution)/shard_map/log1p | solution.py:610
